TPU v7x, 768 devices: a whole 4x8x12 slice. The times are simulated.
768 devices in a mesh: gx: 96 (over y, z), gy: 8 (over x, core).
Axes of the slice: x: 4, y: 8, z: 12, core: 2. Of those that a mesh axis runs over, the one named last changes fastest.
Arguments:
- ice_rhs: float32 [2, 6144, 2048], P(None, 'gx', 'gy'), may hold values from -18.6 to 18.6
- ice_guess: float32 [2, 6144, 2048], P(None, 'gx', 'gy'), may hold values from -9.3 to 9.3
- ocean_rhs: float32 [6144, 2048], P('gx', 'gy'), may hold values from -18.6 to 18.6
- ocean_guess: float32 [6144, 2048], P('gx', 'gy'), may hold values from -9.3 to 9.3
- ice_diag: float32 [6144, 2048], P('gx', 'gy'), may hold values from 1 to 4
- ice_visc: float32 [6144, 2048], P('gx', 'gy'), may hold values from 0.5 to 1.5
- coriolis: float32 [6144, 2048], P('gx', 'gy'), may hold values from -1.5 to 1.5
- depth_factor: float32 [6144, 2048], P('gx', 'gy'), may hold values from 1 to 3
- wet_mask: int32 [6144, 2048], P('gx', 'gy'), may hold values 0 or 1
- ice_mask: int32 [6144, 2048], P('gx', 'gy'), may hold values from 0 to 1, as said below
Outputs:
- ice_velocity: float32 [2, 6144, 2048], P(None, 'gx', 'gy')
- ocean_level: float32 [6144, 2048], P('gx', 'gy')
Inputs may be any that keep to these rules, and one draw needn't show every extreme that they name: `ice_mask`: 1 where sea ice covers the cell.
All inputs are finite; a program needn't handle non-finite values. No bound on the sum of `wet_mask` on one device may be relied on, other than what follows from the above.
Results may differ from a plain program's by a relative error of at most 0.00005.
Values sent between devices are 32-bit elements; how exact they have to be, the bound alone decides.
A program may use at most 32 MiB of HBM per device.

v0:
```python
import functools

import jax
import jax.numpy as jnp
from jax import lax
from jax.sharding import Mesh
from jax.sharding import PartitionSpec as P

GY = ("gy_0", "gy_1")
GX = ("gx_0", "gx_1")
GX_GY = ("gx_0", "gx_1", "gy_0", "gy_1")


def shifted(value, axis, by):
    size = lax.axis_size(axis)
    pairs = [(i, i + by) for i in range(size) if 0 <= i + by < size]
    return lax.ppermute(value, axis, pairs)


def extended(cells, sides, width, closed):
    for axis, dim in sides:
        count = lax.axis_size(axis)
        ends = count if closed else count - 1
        head = lax.slice_in_dim(cells, 0, width, axis=dim)
        tail = lax.slice_in_dim(cells, cells.shape[dim] - width, cells.shape[dim], axis=dim)
        cells = jnp.concatenate(
            [
                lax.ppermute(tail, axis, [(i, (i + 1) % count) for i in range(ends)]),
                cells,
                lax.ppermute(head, axis, [((i + 1) % count, i) for i in range(ends)]),
            ],
            axis=dim,
        )
    return cells


def by_axis(value, axes):
    return functools.reduce(lax.psum, axes, value)


def inner(left, right):
    return jnp.sum(left * right)


def body(
    ice_rhs,
    ice_guess,
    ocean_rhs,
    ocean_guess,
    ice_diag,
    ice_visc,
    coriolis,
    depth_factor,
    wet_mask,
    ice_mask,
):
    wet = wet_mask.astype(jnp.float32)
    active = wet * ice_mask.astype(jnp.float32)
    act = jnp.stack([active, active, wet])
    root = jnp.stack([ice_visc, ice_visc, depth_factor])
    diag = jnp.stack([ice_diag, ice_diag, jnp.ones_like(ice_diag)])
    inverse = 1.0 / (act * (diag + 4.0 * root * root) + 1.0 - act)
    signs = jnp.array([-1.0, -1.0, 1.0], jnp.float32)[:, None]
    at_top = lax.axis_index(GY) == lax.axis_size(GY) - 1

    def mirror_sections():
        sections = []
        group = lax.axis_size(GX)
        while group % 2 == 0:
            sections.append((group // 2, group, 0))
            group = group // 2
        sections.append((2, group, 1))
        return sections

    def partner_row(q):
        moving = q[:, :, -1]
        position = lax.axis_index(GX)
        for distance, extent, sort_kind in mirror_sections():
            within = position % extent
            from_above = shifted(moving, GX, -distance)
            from_below = shifted(moving, GX, distance)
            if sort_kind == 0:
                take_above = within < distance
                take_below = within >= distance
            else:
                take_above = extent - 1 - 2 * within == distance
                take_below = extent - 1 - 2 * within == -distance
            moving = jnp.where(take_above, from_above, jnp.where(take_below, from_below, moving))
        return moving[:, ::-1]

    def operate(field):
        q = act * root * field
        zonal = extended(q, ((GX, 1),), 1, True)
        merid = extended(q, ((GY, 2),), 1, False)
        ghost = jnp.where(at_top, signs * partner_row(q), 0.0)
        north = jnp.concatenate([merid[:, :, 2:-1], merid[:, :, -1:] + ghost[:, :, None]], axis=2)
        beside_all = zonal[:, 2:, :] + zonal[:, :-2, :] + north + merid[:, :, :-2]
        lap = 4.0 * q - beside_all
        turn = jnp.stack([-coriolis * field[1], coriolis * field[0], jnp.zeros_like(coriolis)])
        return act * (diag * field + root * lap + turn) + (1.0 - act) * field

    start_image = operate(jnp.concatenate([ice_guess, ocean_guess[None]]))
    resid = jnp.concatenate([ice_rhs, ocean_rhs[None]]) - start_image
    r = resid[:2]
    ro = resid[2]
    pre = inverse * resid
    image = operate(pre)
    w_scaled = image[:2]
    az0 = image[2]
    z_scaled = pre[:2]
    z0 = pre[2]

    def merged(values):
        return by_axis(jnp.stack(values), GX_GY)

    sums = merged(
        [inner(r, r), inner(w_scaled, r), inner(w_scaled, w_scaled), inner(ro, z0), inner(z0, az0)]
    )
    rr = sums[0]
    beta = jnp.sqrt(rr)
    h11 = sums[1] / rr
    g11 = sums[2] / rr
    h21 = jnp.sqrt(g11 - h11 * h11)
    gamma0 = sums[3]
    alpha0 = gamma0 / sums[4]
    v2 = (w_scaled - h11 * r) / (beta * h21)
    level = ocean_guess + alpha0 * z0
    ro = ro - alpha0 * az0
    znext = inverse[2] * ro
    image2 = operate(jnp.concatenate([inverse[:2] * v2, znext[None]]))
    w2 = image2[:2]
    sums = merged(
        [inner(w2, r), inner(w2, v2), inner(w2, w2), inner(ro, znext), inner(znext, image2[2])]
    )
    h12 = sums[0] / beta
    h22 = sums[1]
    g22 = sums[2]
    gamma1 = sums[3]
    lead = gamma1 / gamma0
    alpha1 = gamma1 / (sums[4] - lead * gamma1 / alpha0)
    p1 = znext + lead * z0
    level = level + alpha1 * p1
    g12 = h11 * h12 + h21 * h22
    first_rhs = beta * h11
    second_rhs = beta * h12
    det = g11 * g22 - g12 * g12
    y_first = (g22 * first_rhs - g12 * second_rhs) / det
    y_second = (g11 * second_rhs - g12 * first_rhs) / det
    velocity = ice_guess + y_first * (z_scaled / beta) + y_second * (inverse[:2] * v2)
    return (velocity, level)


def solution(mesh):
    torus = Mesh(mesh.devices.reshape(8, 12, 4, 2), ("gx_0", "gx_1", "gy_0", "gy_1"))
    in_specs = (
        P(None, GX, GY),
        P(None, GX, GY),
        P(GX, GY),
        P(GX, GY),
        P(GX, GY),
        P(GX, GY),
        P(GX, GY),
        P(GX, GY),
        P(GX, GY),
        P(GX, GY),
    )
    out_specs = (P(None, GX, GY), P(GX, GY))
    return jax.shard_map(body, mesh=torus, in_specs=in_specs, out_specs=out_specs, check_vma=False)
```

profile of v0, /device:TPU:1, one launch (start us, length us, event | category | flops | bytes accessed | tf_op | source)
XLA Modules:
  0.0 386.6 jit_solution(222065659185932568)
XLA Ops:
  4.0 8.3 %collective-permute-start.4 = (f32[3,64]{1,0:T(4,128)S(1)}, f32[3,64]{1,0:T(4,128)S(1)}, u32[]{:S(2)}, u32[]{:S(2)}) collective-permute-start(f32[3,64]{1,0:T(4,128)S(1)} %get-tuple-element.39), channel_id=1, source_target_pairs={{0,384},{8,392},{16,400},{24,408},{32,416},{40,424},{48,432},{56,4... | collective-permute-start | bytes 2312 | tf_op jit(solution)/shard_map/ppermute | solution.py:17
  12.3 12.6 %collective-permute-start.2 = (f32[3,64,1]{2,1,0:T(8,128)S(1)}, f32[3,64,1]{2,1,0:T(8,128)S(1)}, u32[]{:S(2)}, u32[]{:S(2)}) collective-permute-start(f32[3,64,1]{2,1,0:T(8,128)S(1)} %get-tuple-element.41), channel_id=1, source_target_pairs={{1,0},{2,1},{3,2},{4,3},{5,4},{6,5},{7,6},{9,8},{10,9},{11,10},{12... | collective-permute-start | bytes 2312 | tf_op jit(solution)/shard_map/ppermute | solution.py:30
  26.8 5.6 %collective-permute-start = (f32[3,1,256]{2,1,0:T(1,128)S(1)}, f32[3,1,256]{2,1,0:T(1,128)S(1)}, u32[]{:S(2)}, u32[]{:S(2)}) collective-permute-start(f32[3,1,256]{2,1,0:T(1,128)S(1)} %get-tuple-element.37), channel_id=1, source_target_pairs={{8,0},{16,8},{24,16},{32,24},{40,32},{48,40},{56,48},{64,56},{72,6... | collective-permute-start | bytes 9224 | tf_op jit(solution)/shard_map/ppermute | solution.py:30
  33.8 5.6 %collective-permute-start.6 = (f32[3,64]{1,0:T(4,128)S(1)}, f32[3,64]{1,0:T(4,128)S(1)}, u32[]{:S(2)}, u32[]{:S(2)}) collective-permute-start(f32[3,64]{1,0:T(4,128)S(1)} %select_select_fusion.17), channel_id=1, source_target_pairs={{0,192},{8,200},{16,208},{24,216},{32,224},{40,232},{48,240},{56,2... | collective-permute-start | bytes 2312 | tf_op jit(solution)/shard_map/ppermute | solution.py:17
  50.1 10.7 %collective-permute-done.9 = f32[3,64]{1,0:T(4,128)S(1)} collective-permute-done((f32[3,64]{1,0:T(4,128)S(1)}, f32[3,64]{1,0:T(4,128)S(1)}, u32[]{:S(2)}, u32[]{:S(2)}) %collective-permute-start.9) | collective-permute-done | bytes 800 | tf_op jit(solution)/shard_map/ppermute | solution.py:17
  62.0 5.8 %collective-permute-start.12 = (f32[3,64]{1,0:T(4,128)S(1)}, f32[3,64]{1,0:T(4,128)S(1)}, u32[]{:S(2)}, u32[]{:S(2)}) collective-permute-start(f32[3,64]{1,0:T(4,128)S(1)} %select_select_fusion.14), channel_id=1, source_target_pairs={{0,24},{8,32},{16,40},{24,48},{32,56},{40,64},{48,72},{56,80},{64,... | collective-permute-start | bytes 2312 | tf_op jit(solution)/shard_map/ppermute | solution.py:17
  87.0 14.9 %collective-permute-start.20 = (f32[3,64]{1,0:T(4,128)S(1)}, f32[3,64]{1,0:T(4,128)S(1)}, u32[]{:S(2)}, u32[]{:S(2)}) collective-permute-start(f32[3,64]{1,0:T(4,128)S(1)} %get-tuple-element.32), channel_id=1, source_target_pairs={{0,384},{8,392},{16,400},{24,408},{32,416},{40,424},{48,432},{56,4... | collective-permute-start | bytes 2312 | tf_op jit(solution)/shard_map/ppermute | solution.py:17
  116.8 10.3 %collective-permute-start.26 = (f32[3,64]{1,0:T(4,128)S(1)}, f32[3,64]{1,0:T(4,128)S(1)}, u32[]{:S(2)}, u32[]{:S(2)}) collective-permute-start(f32[3,64]{1,0:T(4,128)S(1)} %select_select_fusion.9), channel_id=1, source_target_pairs={{0,48},{8,56},{16,64},{24,72},{32,80},{40,88},{48,96},{56,104},{64... | collective-permute-start | bytes 2312 | tf_op jit(solution)/shard_map/ppermute | solution.py:17
  127.1 13.2 %collective-permute-start.31 = (f32[3,64,1]{2,1,0:T(8,128)S(1)}, f32[3,64,1]{2,1,0:T(8,128)S(1)}, u32[]{:S(2)}, u32[]{:S(2)}) collective-permute-start(f32[3,64,1]{2,1,0:T(8,128)S(1)} %get-tuple-element.33), channel_id=1, source_target_pairs={{0,1},{1,2},{2,3},{3,4},{4,5},{5,6},{6,7},{8,9},{9,10},{10,11},{11... | collective-permute-start | bytes 2312 | tf_op jit(solution)/shard_map/ppermute | solution.py:28
  141.7 5.8 %collective-permute-start.28 = (f32[3,64]{1,0:T(4,128)S(1)}, f32[3,64]{1,0:T(4,128)S(1)}, u32[]{:S(2)}, u32[]{:S(2)}) collective-permute-start(f32[3,64]{1,0:T(4,128)S(1)} %select_select_fusion.8), channel_id=1, source_target_pairs={{0,24},{8,32},{16,40},{24,48},{32,56},{40,64},{48,72},{56,80},{64,... | collective-permute-start | bytes 2312 | tf_op jit(solution)/shard_map/ppermute | solution.py:17
  155.8 9.7 %collective-permute-start.16 = (f32[3,1,256]{2,1,0:T(1,128)S(1)}, f32[3,1,256]{2,1,0:T(1,128)S(1)}, u32[]{:S(2)}, u32[]{:S(2)}) collective-permute-start(f32[3,1,256]{2,1,0:T(1,128)S(1)} %get-tuple-element.35), channel_id=1, source_target_pairs={{8,0},{16,8},{24,16},{32,24},{40,32},{48,40},{56,48},{64,56},{72,6... | collective-permute-start | bytes 9224 | tf_op jit(solution)/shard_map/ppermute | solution.py:30
  177.9 17.2 %psum.56 = f32[5]{0:T(128)S(1)} all-reduce(f32[5]{0:T(128)S(1)} %stack.109), channel_id=1, replica_groups=mesh['gx_0'=8,'gx_1'=12,'gy_0'=4,'gy_1'=2] {'gx_0'}, use_global_device_ids=true, to_apply=%region_5.6 | all-reduce | flops 5 | bytes 40 | tf_op jit(solution)/shard_map/psum | solution.py:38
  195.2 15.4 %psum.57 = f32[5]{0:T(128)S(1)} all-reduce(f32[5]{0:T(128)S(1)} %psum.56), channel_id=1, replica_groups=mesh['gx_0'=8,'gx_1'=12,'gy_0'=4,'gy_1'=2] {'gx_1'}, use_global_device_ids=true, to_apply=%region_6.7 | all-reduce | flops 5 | bytes 40 | tf_op jit(solution)/shard_map/psum | solution.py:38
  210.6 8.4 %psum.58 = f32[5]{0:T(128)S(1)} all-reduce(f32[5]{0:T(128)S(1)} %psum.57), channel_id=1, replica_groups=mesh['gx_0'=8,'gx_1'=12,'gy_0'=4,'gy_1'=2] {'gy_0'}, use_global_device_ids=true, to_apply=%region_7.8 | all-reduce | flops 5 | bytes 40 | tf_op jit(solution)/shard_map/psum | solution.py:38
  219.0 15.1 %psum.59 = f32[5]{0:T(128)S(1)} all-reduce(f32[5]{0:T(128)S(1)} %psum.58), channel_id=1, replica_groups=mesh['gx_0'=8,'gx_1'=12,'gy_0'=4,'gy_1'=2] {'gy_1'}, use_global_device_ids=true, to_apply=%region_8.9 | all-reduce | flops 5 | bytes 40 | tf_op jit(solution)/shard_map/psum | solution.py:38
  240.9 7.9 %collective-permute-start.36 = (f32[3,64]{1,0:T(4,128)S(1)}, f32[3,64]{1,0:T(4,128)S(1)}, u32[]{:S(2)}, u32[]{:S(2)}) collective-permute-start(f32[3,64]{1,0:T(4,128)S(1)} %get-tuple-element.27), channel_id=1, source_target_pairs={{0,384},{8,392},{16,400},{24,408},{32,416},{40,424},{48,432},{56,4... | collective-permute-start | bytes 2312 | tf_op jit(solution)/shard_map/ppermute | solution.py:17
  263.7 10.3 %collective-permute-start.42 = (f32[3,64]{1,0:T(4,128)S(1)}, f32[3,64]{1,0:T(4,128)S(1)}, u32[]{:S(2)}, u32[]{:S(2)}) collective-permute-start(f32[3,64]{1,0:T(4,128)S(1)} %select_select_fusion.3), channel_id=1, source_target_pairs={{0,48},{8,56},{16,64},{24,72},{32,80},{40,88},{48,96},{56,104},{64... | collective-permute-start | bytes 2312 | tf_op jit(solution)/shard_map/ppermute | solution.py:17
  276.0 5.8 %collective-permute-start.44 = (f32[3,64]{1,0:T(4,128)S(1)}, f32[3,64]{1,0:T(4,128)S(1)}, u32[]{:S(2)}, u32[]{:S(2)}) collective-permute-start(f32[3,64]{1,0:T(4,128)S(1)} %select_select_fusion.2), channel_id=1, source_target_pairs={{0,24},{8,32},{16,40},{24,48},{32,56},{40,64},{48,72},{56,80},{64,... | collective-permute-start | bytes 2312 | tf_op jit(solution)/shard_map/ppermute | solution.py:17
  288.8 8.5 %collective-permute-start.34 = (f32[3,64,1]{2,1,0:T(8,128)S(1)}, f32[3,64,1]{2,1,0:T(8,128)S(1)}, u32[]{:S(2)}, u32[]{:S(2)}) collective-permute-start(f32[3,64,1]{2,1,0:T(8,128)S(1)} %get-tuple-element.29), channel_id=1, source_target_pairs={{1,0},{2,1},{3,2},{4,3},{5,4},{6,5},{7,6},{9,8},{10,9},{11,10},{12... | collective-permute-start | bytes 2312 | tf_op jit(solution)/shard_map/ppermute | solution.py:30
  299.3 16.5 %collective-permute-start.32 = (f32[3,1,256]{2,1,0:T(1,128)S(1)}, f32[3,1,256]{2,1,0:T(1,128)S(1)}, u32[]{:S(2)}, u32[]{:S(2)}) collective-permute-start(f32[3,1,256]{2,1,0:T(1,128)S(1)} %get-tuple-element.30), channel_id=1, source_target_pairs={{8,0},{16,8},{24,16},{32,24},{40,32},{48,40},{56,48},{64,56},{72,6... | collective-permute-start | bytes 9224 | tf_op jit(solution)/shard_map/ppermute | solution.py:30
  328.1 13.4 %psum.60 = f32[5]{0:T(128)S(1)} all-reduce(f32[5]{0:T(128)S(1)} %stack.118), channel_id=1, replica_groups=mesh['gx_0'=8,'gx_1'=12,'gy_0'=4,'gy_1'=2] {'gx_0'}, use_global_device_ids=true, to_apply=%region_14.15 | all-reduce | flops 5 | bytes 40 | tf_op jit(solution)/shard_map/psum | solution.py:38
  341.5 15.9 %psum.61 = f32[5]{0:T(128)S(1)} all-reduce(f32[5]{0:T(128)S(1)} %psum.60), channel_id=1, replica_groups=mesh['gx_0'=8,'gx_1'=12,'gy_0'=4,'gy_1'=2] {'gx_1'}, use_global_device_ids=true, to_apply=%region_15.16 | all-reduce | flops 5 | bytes 40 | tf_op jit(solution)/shard_map/psum | solution.py:38
  357.4 6.2 %psum.62 = f32[5]{0:T(128)S(1)} all-reduce(f32[5]{0:T(128)S(1)} %psum.61), channel_id=1, replica_groups=mesh['gx_0'=8,'gx_1'=12,'gy_0'=4,'gy_1'=2] {'gy_0'}, use_global_device_ids=true, to_apply=%region_16.17 | all-reduce | flops 5 | bytes 40 | tf_op jit(solution)/shard_map/psum | solution.py:38
  363.6 14.0 %psum.63 = f32[5]{0:T(128)S(1)} all-reduce(f32[5]{0:T(128)S(1)} %psum.62), channel_id=1, replica_groups=mesh['gx_0'=8,'gx_1'=12,'gy_0'=4,'gy_1'=2] {'gy_1'}, use_global_device_ids=true, to_apply=%region_17.18 | all-reduce | flops 5 | bytes 40 | tf_op jit(solution)/shard_map/psum | solution.py:38
  (161 shorter events, 116.3 us)
Async XLA Ops:
  2.7 29.7 %collective-permute-start.3 = (f32[3,64]{1,0:T(4,128)S(1)}, f32[3,64]{1,0:T(4,128)S(1)}, u32[]{:S(2)}, u32[]{:S(2)}) collective-permute-start(f32[3,64]{1,0:T(4,128)S(1)} %get-tuple-element.39), channel_id=1, source_target_pairs={{384,0},{392,8},{400,16},{408,24},{416,32},{424,40},{432,48},{440,... | collective-permute-start | bytes 2312 | tf_op jit(solution)/shard_map/ppermute | solution.py:17
  4.0 28.4 %collective-permute-start.4 = (f32[3,64]{1,0:T(4,128)S(1)}, f32[3,64]{1,0:T(4,128)S(1)}, u32[]{:S(2)}, u32[]{:S(2)}) collective-permute-start(f32[3,64]{1,0:T(4,128)S(1)} %get-tuple-element.39), channel_id=1, source_target_pairs={{0,384},{8,392},{16,400},{24,408},{32,416},{40,424},{48,432},{56,4... | collective-permute-start | bytes 2312 | tf_op jit(solution)/shard_map/ppermute | solution.py:17
  12.3 68.4 %collective-permute-start.2 = (f32[3,64,1]{2,1,0:T(8,128)S(1)}, f32[3,64,1]{2,1,0:T(8,128)S(1)}, u32[]{:S(2)}, u32[]{:S(2)}) collective-permute-start(f32[3,64,1]{2,1,0:T(8,128)S(1)} %get-tuple-element.41), channel_id=1, source_target_pairs={{1,0},{2,1},{3,2},{4,3},{5,4},{6,5},{7,6},{9,8},{10,9},{11,10},{12... | collective-permute-start | bytes 2312 | tf_op jit(solution)/shard_map/ppermute | solution.py:30
  24.9 55.9 %collective-permute-start.15 = (f32[3,64,1]{2,1,0:T(8,128)S(1)}, f32[3,64,1]{2,1,0:T(8,128)S(1)}, u32[]{:S(2)}, u32[]{:S(2)}) collective-permute-start(f32[3,64,1]{2,1,0:T(8,128)S(1)} %get-tuple-element.40), channel_id=1, source_target_pairs={{0,1},{1,2},{2,3},{3,4},{4,5},{5,6},{6,7},{8,9},{9,10},{10,11},{11... | collective-permute-start | bytes 2312 | tf_op jit(solution)/shard_map/ppermute | solution.py:28
  26.8 53.9 %collective-permute-start = (f32[3,1,256]{2,1,0:T(1,128)S(1)}, f32[3,1,256]{2,1,0:T(1,128)S(1)}, u32[]{:S(2)}, u32[]{:S(2)}) collective-permute-start(f32[3,1,256]{2,1,0:T(1,128)S(1)} %get-tuple-element.37), channel_id=1, source_target_pairs={{8,0},{16,8},{24,16},{32,24},{40,32},{48,40},{56,48},{64,56},{72,6... | collective-permute-start | bytes 9224 | tf_op jit(solution)/shard_map/ppermute | solution.py:30
  48.7 12.0 %collective-permute-start.9 = (f32[3,64]{1,0:T(4,128)S(1)}, f32[3,64]{1,0:T(4,128)S(1)}, u32[]{:S(2)}, u32[]{:S(2)}) collective-permute-start(f32[3,64]{1,0:T(4,128)S(1)} %select_select_fusion.15), channel_id=1, source_target_pairs={{48,0},{56,8},{64,16},{72,24},{80,32},{88,40},{96,48},{104,56},{11... | collective-permute-start | bytes 2312 | tf_op jit(solution)/shard_map/ppermute | solution.py:17
  69.8 10.0 %collective-permute-start.14 = (f32[3,64]{1,0:T(4,128)S(1)}, f32[3,64]{1,0:T(4,128)S(1)}, u32[]{:S(2)}, u32[]{:S(2)}) collective-permute-start(f32[3,64]{1,0:T(4,128)S(1)} %select_select_fusion.13), channel_id=1, source_target_pairs={{0,16},{8,24},{16,32},{24,40},{32,48},{40,56},{48,64},{56,72},{64,... | collective-permute-start | bytes 2312 | tf_op jit(solution)/shard_map/ppermute | solution.py:17
  75.3 9.9 %collective-permute-start.1 = (f32[3,1,256]{2,1,0:T(1,128)S(1)}, f32[3,1,256]{2,1,0:T(1,128)S(1)}, u32[]{:S(2)}, u32[]{:S(2)}) collective-permute-start(f32[3,1,256]{2,1,0:T(1,128)S(1)} %get-tuple-element.38), channel_id=1, source_target_pairs={{0,8},{8,16},{16,24},{24,32},{32,40},{40,48},{48,56},{56,64},{64,7... | collective-permute-start | bytes 9224 | tf_op jit(solution)/shard_map/ppermute | solution.py:28
  85.7 16.2 %collective-permute-start.19 = (f32[3,64]{1,0:T(4,128)S(1)}, f32[3,64]{1,0:T(4,128)S(1)}, u32[]{:S(2)}, u32[]{:S(2)}) collective-permute-start(f32[3,64]{1,0:T(4,128)S(1)} %get-tuple-element.32), channel_id=1, source_target_pairs={{384,0},{392,8},{400,16},{408,24},{416,32},{424,40},{432,48},{440,... | collective-permute-start | bytes 2312 | tf_op jit(solution)/shard_map/ppermute | solution.py:17
  87.0 15.6 %collective-permute-start.20 = (f32[3,64]{1,0:T(4,128)S(1)}, f32[3,64]{1,0:T(4,128)S(1)}, u32[]{:S(2)}, u32[]{:S(2)}) collective-permute-start(f32[3,64]{1,0:T(4,128)S(1)} %get-tuple-element.32), channel_id=1, source_target_pairs={{0,384},{8,392},{16,400},{24,408},{32,416},{40,424},{48,432},{56,4... | collective-permute-start | bytes 2312 | tf_op jit(solution)/shard_map/ppermute | solution.py:17
  115.5 24.8 %collective-permute-start.25 = (f32[3,64]{1,0:T(4,128)S(1)}, f32[3,64]{1,0:T(4,128)S(1)}, u32[]{:S(2)}, u32[]{:S(2)}) collective-permute-start(f32[3,64]{1,0:T(4,128)S(1)} %select_select_fusion.9), channel_id=1, source_target_pairs={{48,0},{56,8},{64,16},{72,24},{80,32},{88,40},{96,48},{104,56},{11... | collective-permute-start | bytes 2312 | tf_op jit(solution)/shard_map/ppermute | solution.py:17
  116.8 23.6 %collective-permute-start.26 = (f32[3,64]{1,0:T(4,128)S(1)}, f32[3,64]{1,0:T(4,128)S(1)}, u32[]{:S(2)}, u32[]{:S(2)}) collective-permute-start(f32[3,64]{1,0:T(4,128)S(1)} %select_select_fusion.9), channel_id=1, source_target_pairs={{0,48},{8,56},{16,64},{24,72},{32,80},{40,88},{48,96},{56,104},{64... | collective-permute-start | bytes 2312 | tf_op jit(solution)/shard_map/ppermute | solution.py:17
  127.1 40.6 %collective-permute-start.31 = (f32[3,64,1]{2,1,0:T(8,128)S(1)}, f32[3,64,1]{2,1,0:T(8,128)S(1)}, u32[]{:S(2)}, u32[]{:S(2)}) collective-permute-start(f32[3,64,1]{2,1,0:T(8,128)S(1)} %get-tuple-element.33), channel_id=1, source_target_pairs={{0,1},{1,2},{2,3},{3,4},{4,5},{5,6},{6,7},{8,9},{9,10},{10,11},{11... | collective-permute-start | bytes 2312 | tf_op jit(solution)/shard_map/ppermute | solution.py:28
  147.6 20.1 %collective-permute-start.18 = (f32[3,64,1]{2,1,0:T(8,128)S(1)}, f32[3,64,1]{2,1,0:T(8,128)S(1)}, u32[]{:S(2)}, u32[]{:S(2)}) collective-permute-start(f32[3,64,1]{2,1,0:T(8,128)S(1)} %get-tuple-element.34), channel_id=1, source_target_pairs={{1,0},{2,1},{3,2},{4,3},{5,4},{6,5},{7,6},{9,8},{10,9},{11,10},{12... | collective-permute-start | bytes 2312 | tf_op jit(solution)/shard_map/ppermute | solution.py:30
  149.6 15.9 %collective-permute-start.29 = (f32[3,64]{1,0:T(4,128)S(1)}, f32[3,64]{1,0:T(4,128)S(1)}, u32[]{:S(2)}, u32[]{:S(2)}) collective-permute-start(f32[3,64]{1,0:T(4,128)S(1)} %select_select_fusion.7), channel_id=1, source_target_pairs={{16,0},{24,8},{32,16},{40,24},{48,32},{56,40},{64,48},{72,56},{80,... | collective-permute-start | bytes 2312 | tf_op jit(solution)/shard_map/ppermute | solution.py:17
  150.9 16.5 %collective-permute-start.30 = (f32[3,64]{1,0:T(4,128)S(1)}, f32[3,64]{1,0:T(4,128)S(1)}, u32[]{:S(2)}, u32[]{:S(2)}) collective-permute-start(f32[3,64]{1,0:T(4,128)S(1)} %select_select_fusion.7), channel_id=1, source_target_pairs={{0,16},{8,24},{16,32},{24,40},{32,48},{40,56},{48,64},{56,72},{64,... | collective-permute-start | bytes 2312 | tf_op jit(solution)/shard_map/ppermute | solution.py:17
  155.8 12.0 %collective-permute-start.16 = (f32[3,1,256]{2,1,0:T(1,128)S(1)}, f32[3,1,256]{2,1,0:T(1,128)S(1)}, u32[]{:S(2)}, u32[]{:S(2)}) collective-permute-start(f32[3,1,256]{2,1,0:T(1,128)S(1)} %get-tuple-element.35), channel_id=1, source_target_pairs={{8,0},{16,8},{24,16},{32,24},{40,32},{48,40},{56,48},{64,56},{72,6... | collective-permute-start | bytes 9224 | tf_op jit(solution)/shard_map/ppermute | solution.py:30
  262.4 11.6 %collective-permute-start.41 = (f32[3,64]{1,0:T(4,128)S(1)}, f32[3,64]{1,0:T(4,128)S(1)}, u32[]{:S(2)}, u32[]{:S(2)}) collective-permute-start(f32[3,64]{1,0:T(4,128)S(1)} %select_select_fusion.3), channel_id=1, source_target_pairs={{48,0},{56,8},{64,16},{72,24},{80,32},{88,40},{96,48},{104,56},{11... | collective-permute-start | bytes 2312 | tf_op jit(solution)/shard_map/ppermute | solution.py:17
  263.7 11.0 %collective-permute-start.42 = (f32[3,64]{1,0:T(4,128)S(1)}, f32[3,64]{1,0:T(4,128)S(1)}, u32[]{:S(2)}, u32[]{:S(2)}) collective-permute-start(f32[3,64]{1,0:T(4,128)S(1)} %select_select_fusion.3), channel_id=1, source_target_pairs={{0,48},{8,56},{16,64},{24,72},{32,80},{40,88},{48,96},{56,104},{64... | collective-permute-start | bytes 2312 | tf_op jit(solution)/shard_map/ppermute | solution.py:17
  282.5 33.2 %collective-permute-start.45 = (f32[3,64]{1,0:T(4,128)S(1)}, f32[3,64]{1,0:T(4,128)S(1)}, u32[]{:S(2)}, u32[]{:S(2)}) collective-permute-start(f32[3,64]{1,0:T(4,128)S(1)} %select_select_fusion.1), channel_id=1, source_target_pairs={{16,0},{24,8},{32,16},{40,24},{48,32},{56,40},{64,48},{72,56},{80,... | collective-permute-start | bytes 2312 | tf_op jit(solution)/shard_map/ppermute | solution.py:17
  283.8 33.9 %collective-permute-start.46 = (f32[3,64]{1,0:T(4,128)S(1)}, f32[3,64]{1,0:T(4,128)S(1)}, u32[]{:S(2)}, u32[]{:S(2)}) collective-permute-start(f32[3,64]{1,0:T(4,128)S(1)} %select_select_fusion.1), channel_id=1, source_target_pairs={{0,16},{8,24},{16,32},{24,40},{32,48},{40,56},{48,64},{56,72},{64,... | collective-permute-start | bytes 2312 | tf_op jit(solution)/shard_map/ppermute | solution.py:17
  288.8 29.2 %collective-permute-start.34 = (f32[3,64,1]{2,1,0:T(8,128)S(1)}, f32[3,64,1]{2,1,0:T(8,128)S(1)}, u32[]{:S(2)}, u32[]{:S(2)}) collective-permute-start(f32[3,64,1]{2,1,0:T(8,128)S(1)} %get-tuple-element.29), channel_id=1, source_target_pairs={{1,0},{2,1},{3,2},{4,3},{5,4},{6,5},{7,6},{9,8},{10,9},{11,10},{12... | collective-permute-start | bytes 2312 | tf_op jit(solution)/shard_map/ppermute | solution.py:30
  297.3 20.7 %collective-permute-start.47 = (f32[3,64,1]{2,1,0:T(8,128)S(1)}, f32[3,64,1]{2,1,0:T(8,128)S(1)}, u32[]{:S(2)}, u32[]{:S(2)}) collective-permute-start(f32[3,64,1]{2,1,0:T(8,128)S(1)} %get-tuple-element.28), channel_id=1, source_target_pairs={{0,1},{1,2},{2,3},{3,4},{4,5},{5,6},{6,7},{8,9},{9,10},{10,11},{11... | collective-permute-start | bytes 2312 | tf_op jit(solution)/shard_map/ppermute | solution.py:28
  299.3 18.8 %collective-permute-start.32 = (f32[3,1,256]{2,1,0:T(1,128)S(1)}, f32[3,1,256]{2,1,0:T(1,128)S(1)}, u32[]{:S(2)}, u32[]{:S(2)}) collective-permute-start(f32[3,1,256]{2,1,0:T(1,128)S(1)} %get-tuple-element.30), channel_id=1, source_target_pairs={{8,0},{16,8},{24,16},{32,24},{40,32},{48,40},{56,48},{64,56},{72,6... | collective-permute-start | bytes 9224 | tf_op jit(solution)/shard_map/ppermute | solution.py:30
  (33 other events, 211.7 us)
where the time goes:
time: 388 us; the launch traced here: 387 us
  starting transfers between devices  217 us (56%)
  blocking collectives  106 us (27%)
  waiting for transfers between devices  33.5 us (9%)
  between operations  13.3 us (3%)
  local copies, waits for them, and re-layouts  9.88 us (3%)
  other arithmetic  6.99 us (2%)
    ppermute x36, starting transfers between devices, shifted(): return lax.ppermute(value, axis, pairs)  137 us
    psum x8, blocking collectives, by_axis(): return functools.reduce(lax.psum, axes, value)  106 us
    ppermute x6, starting transfers between devices, extended(): lax.ppermute(head, axis, [((i + 1) % count, i) for i in range(ends)])  54.7 us
    ppermute x6, starting transfers between devices, extended(): lax.ppermute(tail, axis, [(i, (i + 1) % count) for i in range(ends)])  25.4 us
    ppermute x36, waiting for transfers between devices, shifted(): return lax.ppermute(value, axis, pairs)  18.3 us
    ppermute x6, waiting for transfers between devices, extended(): lax.ppermute(tail, axis, [(i, (i + 1) % count) for i in range(ends)])  15.2 us
  transfers between devices with their start and end apart: 48, of which 15 were waited for; matrix products, arithmetic and copies ran while one was open for 0% of the time, Pallas kernels for 0%

commit v1 on v0

v1 whole, which is shorter than its diff:
```python
import functools

import jax
import jax.numpy as jnp
from jax import lax
from jax.experimental import pallas as pl
from jax.experimental.pallas import tpu as pltpu
from jax.sharding import PartitionSpec as P

MESH = pl.DeviceIdType.MESH

M_U, M_V, H_U, H_V, M_O, H_O, B_I, B_O, TURN = range(9)
GROUPS = ((M_U, M_V, H_U, H_V, M_O), (H_O, B_I, B_O, TURN))
PACK = 48
ROWS = 64
COLS = 256
EXT_ROWS = ROWS + 8
EXT_COLS = COLS + 128


def iota(shape, dim):
    return lax.broadcasted_iota(jnp.int32, shape, dim)


def around(q):
    rows, cols = q.shape
    return (
        pltpu.roll(q, 1, 0) + pltpu.roll(q, rows - 1, 0) + pltpu.roll(q, 1, 1) + pltpu.roll(q, cols - 1, 1)
    )


def inner_block(x):
    return x[:ROWS, :COLS]


def kernel(
    sizes,
    ice_rhs,
    ice_guess,
    ocean_rhs,
    ocean_guess,
    ice_diag,
    ice_visc,
    coriolis,
    depth_factor,
    wet_mask,
    ice_mask,
    velocity,
    level,
    v_rhs,
    v_guess,
    v_orhs,
    v_oguess,
    v_diag,
    v_visc,
    v_cor,
    v_depth,
    v_wet,
    v_ice,
    fields,
    local,
    zonal_out,
    zonal_in,
    merid_out,
    merid_in,
    sum_gy,
    sum_z,
    sum_y,
    load_sems,
    halo_send,
    halo_recv,
    gy_send,
    gy_recv,
    z_send,
    z_recv,
    y_send,
    y_recv,
):
    ny, nz, ngy = sizes
    ngx = ny * nz
    gx = lax.axis_index("gx")
    gy = lax.axis_index("gy")
    yy = gx // nz
    zz = lax.rem(gx, nz)
    top = gy == ngy - 1
    bottom = gy == 0

    loads = []
    for i, (src, dst) in enumerate(
        (
            (ice_rhs, v_rhs),
            (ice_guess, v_guess),
            (ocean_rhs, v_orhs),
            (ocean_guess, v_oguess),
            (ice_diag, v_diag),
            (ice_visc, v_visc),
            (coriolis, v_cor),
            (depth_factor, v_depth),
            (wet_mask, v_wet),
            (ice_mask, v_ice),
        )
    ):
        loads.append(pltpu.make_async_copy(src, dst, load_sems.at[i]))

    def wrap(x):
        return lax.rem(x + ngx, ngx)

    def north_of(step):
        there = wrap(gx + step)
        return jnp.where(top, ngx - 1 - there, there), jnp.where(top, gy, gy + 1)

    def south_of(step):
        return wrap(gx + step), jnp.where(bottom, gy, gy - 1)

    east = (wrap(gx + 1), gy)
    west = (wrap(gx - 1), gy)
    norths = [north_of(step) for step in (0, 1, -1)]
    souths = [south_of(step) for step in (0, 1, -1)]
    gy_peers = [lax.rem(gy + d, ngy) for d in range(1, ngy)]
    z_peers = [lax.rem(zz + d, nz) for d in range(1, nz)]
    y_peers = [lax.rem(yy + d, ny) for d in range(1, ny)]

    barrier = pltpu.get_barrier_semaphore()

    def greet(device):
        pl.semaphore_signal(barrier, inc=1, device_id=device, device_id_type=MESH)

    mirror_self = [jnp.logical_and(top, norths[k][0] == gx) for k in (1, 2)]

    greet(norths[0])
    for k in (1, 2):

        @pl.when(jnp.logical_not(mirror_self[k - 1]))
        def _():
            greet(norths[k])

    for p in z_peers:
        greet((yy * nz + p, gy))
    for p in y_peers:
        greet((p * nz + zz, gy))
    for p in gy_peers:
        greet((gx, p))
    greet(east)
    greet(west)

    @pl.when(jnp.logical_not(bottom))
    def _():
        for device in souths:
            greet(device)

    for copy in loads:
        copy.start()
    for copy in loads:
        copy.wait()

    wet = v_wet[...].astype(jnp.float32)
    active = wet * v_ice[...].astype(jnp.float32)
    visc = v_visc[...]
    depth = v_depth[...]
    d_i = active * (v_diag[...] + 4.0 * visc * visc) + 1.0 - active
    d_o = wet * (1.0 + 4.0 * depth * depth) + 1.0 - wet
    p_i = 1.0 / d_i
    p_o = 1.0 / d_o
    r_i = active * visc
    r_o = wet * depth
    s_i = r_i * p_i
    s_o = r_o * p_o
    c = active * v_cor[...]
    g_u = v_guess[0]
    g_v = v_guess[1]
    g_o = v_oguess[...]
    h_u = v_rhs[0] - d_i * g_u + c * g_v
    h_v = v_rhs[1] - d_i * g_v - c * g_u
    h_o = v_orhs[...] - d_o * g_o
    own = {
        M_U: r_i * g_u,
        M_V: r_i * g_v,
        M_O: r_o * g_o,
        H_U: s_i * h_u,
        H_V: s_i * h_v,
        H_O: s_o * h_o,
        B_I: r_i * s_i,
        B_O: r_o * s_o,
        TURN: c * p_i,
    }
    for k, value in enumerate((h_u, h_v, h_o, r_i, r_o, p_i, p_o)):
        local[k] = value
    for f in range(9):
        fields[f, 0:ROWS, 0:COLS] = own[f]

    sub = iota((8, COLS), 0)
    for t in range(5):
        a, b = 2 * t, min(2 * t + 1, 8)
        first_a, last_a = own[a][0:8], own[a][ROWS - 8 : ROWS]
        first_b, last_b = own[b][0:8], own[b][ROWS - 8 : ROWS]
        zonal_out[0, t] = jnp.where(sub >= 4, last_a, pltpu.roll(last_b, 3, 0))
        zonal_out[1, t] = jnp.where(sub < 4, first_a, pltpu.roll(first_b, 5, 0))

    lane = iota((ROWS, 128), 1)
    halves = []
    for group in GROUPS:
        packed = jnp.zeros((ROWS, 128), jnp.float32)
        for k, f in enumerate(group):
            edge = jnp.where(lane < 64, own[f][:, 0:128], own[f][:, COLS - 128 : COLS])
            moved = pltpu.roll(edge, 8 * (k + 1), 1)
            packed = jnp.where(jnp.logical_and(lane >= 8 * k + 4, lane < 8 * k + 12), moved, packed)
        halves.append(packed)
    turned = jnp.transpose(jnp.concatenate(halves, axis=0))[0:PACK]
    merid_out[0] = turned
    merid_out[1] = turned

    @pl.when(top)
    def _():
        row = iota((PACK, 128), 0)
        within = lax.rem(row, 8)
        flipped = jnp.where(
            within == 0,
            pltpu.roll(turned, 1, 0),
            jnp.where(within == 1, pltpu.roll(turned, 3, 0), pltpu.roll(turned, 5, 0)),
        )
        swap = jnp.where(
            (iota((128, 128), 0) ^ iota((128, 128), 1)) == 63, 1.0, 0.0
        ).astype(jnp.float32)
        mirrored = jnp.dot(
            flipped, swap, precision=lax.Precision.HIGHEST, preferred_element_type=jnp.float32
        )
        minus = jnp.logical_and(row < 40, iota((PACK, 128), 1) < 64)
        merid_out[0] = jnp.where(minus, -mirrored, mirrored)

    @pl.when(bottom)
    def _():
        for k in range(3):
            merid_in[3 + k] = jnp.zeros((PACK, 128), jnp.float32)

    expected = ny + nz + ngy - 3 + 2 + 1 + jnp.where(bottom, 0, 3)
    for k in (1, 2):
        expected = expected + jnp.where(mirror_self[k - 1], 0, 1)
    pl.semaphore_wait(barrier, expected)

    def remote(src, dst, sent, got, device):
        return pltpu.make_async_remote_copy(
            src_ref=src,
            dst_ref=dst,
            send_sem=halo_send.at[sent],
            recv_sem=halo_recv.at[got],
            device_id=device,
            device_id_type=MESH,
        )

    slot_of = (0, 2, 1)
    fold = [remote(merid_out.at[0], merid_in.at[k], k, k, norths[k]) for k in range(3)]
    up = [
        remote(merid_out.at[0], merid_in.at[3 + slot_of[k]], k, 3 + slot_of[k], norths[k])
        for k in range(3)
    ]
    down = [
        remote(merid_out.at[1], merid_in.at[slot_of[k]], 3 + k, slot_of[k], souths[k]) for k in range(3)
    ]
    to_east = remote(zonal_out.at[0], zonal_in.at[0], 6, 6, east)
    to_west = remote(zonal_out.at[1], zonal_in.at[1], 7, 7, west)

    @pl.when(top)
    def _():
        fold[0].start()

    for k in (1, 2):

        @pl.when(jnp.logical_and(top, jnp.logical_not(mirror_self[k - 1])))
        def _():
            fold[k].start()

        @pl.when(mirror_self[k - 1])
        def _():
            merid_in[k] = merid_out[0]

    @pl.when(jnp.logical_not(top))
    def _():
        for copy in up:
            copy.start()

    @pl.when(jnp.logical_not(bottom))
    def _():
        for copy in down:
            copy.start()

    to_east.start()
    to_west.start()

    to_east.wait_recv()
    to_west.wait_recv()

    for t in range(5):
        from_west = zonal_in[0, t]
        from_east = zonal_in[1, t]
        fields[2 * t, ROWS:EXT_ROWS, 0:COLS] = jnp.where(sub < 4, from_east, from_west)
        if t < 4:
            fields[2 * t + 1, ROWS:EXT_ROWS, 0:COLS] = jnp.where(
                sub < 4, pltpu.roll(from_east, 3, 0), pltpu.roll(from_west, 5, 0)
            )

    def arrived(k):
        remote(merid_out.at[0], merid_in.at[k], k, k, east).wait_recv()

    arrived(0)
    for k in (1, 2):

        @pl.when(jnp.logical_not(mirror_self[k - 1]))
        def _():
            arrived(k)

    @pl.when(jnp.logical_not(bottom))
    def _():
        for k in range(3):
            arrived(3 + k)

    north_side = lax.rem(iota((PACK, 128), 0), 8) < 4
    plane, from_e, from_w = [jnp.where(north_side, merid_in[k], merid_in[3 + k]) for k in range(3)]
    lane = iota((PACK, 128), 1)
    pad = jnp.zeros((128 - PACK, 128), jnp.float32)
    for g, group in enumerate(GROUPS):
        if g == 0:
            center, right, left = plane, pltpu.roll(from_e, 64, 1), pltpu.roll(from_w, 8, 1)
        else:
            center, right, left = pltpu.roll(plane, 64, 1), from_e, pltpu.roll(from_w, 72, 1)
        merged = jnp.where(lane < 64, center, jnp.where(lane < 68, right, left))
        back = jnp.transpose(jnp.concatenate([merged, pad], axis=0))[0:EXT_ROWS]
        for k, f in enumerate(group):
            fields[f, :, COLS:EXT_COLS] = pltpu.roll(back, 128 - 8 * (k + 1), 1)

    b_i = fields[B_I]
    b_o = fields[B_O]
    turn = fields[TURN]
    t_in = inner_block(turn)
    h_u, h_v, h_o = local[0], local[1], local[2]
    r_i, r_o, p_i, p_o = local[3], local[4], local[5], local[6]
    nb_u = around(fields[M_U])
    nb_v = around(fields[M_V])
    nb_o = around(fields[M_O])
    s0_u = fields[H_U] + b_i * nb_u
    s0_v = fields[H_V] + b_i * nb_v
    s0_o = fields[H_O] + b_o * nb_o
    res_u = h_u + r_i * inner_block(nb_u)
    res_v = h_v + r_i * inner_block(nb_v)
    res_o = h_o + r_o * inner_block(nb_o)
    nb_u = around(s0_u)
    nb_v = around(s0_v)
    nb_o = around(s0_o)
    s1_u = b_i * nb_u + turn * s0_v
    s1_v = b_i * nb_v - turn * s0_u
    s1_o = b_o * nb_o
    n1_u = r_i * inner_block(nb_u) + t_in * res_v
    n1_v = r_i * inner_block(nb_v) - t_in * res_u
    n1_o = r_o * inner_block(nb_o)
    n2_u = r_i * inner_block(around(s1_u)) + t_in * n1_v
    n2_v = r_i * inner_block(around(s1_v)) - t_in * n1_u
    n2_o = r_o * inner_block(around(s1_o))
    a_u, a_v, a_o = res_u - n1_u, res_v - n1_v, res_o - n1_o
    e_u, e_v, e_o = n1_u - n2_u, n1_v - n2_v, n1_o - n2_o
    z_o = p_o * res_o
    x_o = p_o * n1_o
    products = [
        a_u * a_u + a_v * a_v,
        a_u * e_u + a_v * e_v,
        e_u * e_u + e_v * e_v,
        a_u * res_u + a_v * res_v,
        e_u * res_u + e_v * res_v,
        z_o * a_o,
        x_o * a_o,
        x_o * e_o,
        z_o * res_o,
        x_o * res_o,
    ]
    local[0] = p_i * res_u
    local[1] = p_i * res_v
    local[2] = z_o
    local[3] = p_i * n1_u
    local[4] = p_i * n1_v
    local[5] = x_o

    row = iota((16, 128), 0)
    sums = jnp.zeros((16, 128), jnp.float32)
    for k, product in enumerate(products):
        half = product[:, 0:128] + product[:, 128:256]
        sums = jnp.where(row == k, jnp.sum(half, axis=0, keepdims=True), sums)
    sums = jnp.sum(sums, axis=1, keepdims=True)
    mine = jnp.sum(jnp.where(row == iota((16, 128), 1), sums, 0.0), axis=0, keepdims=True)

    def gather(value, slots, send, recv, me, peers, device_of):
        count = len(peers) + 1
        slots[me] = value
        copies = []
        for d, p in enumerate(peers):
            copy = pltpu.make_async_remote_copy(
                src_ref=slots.at[me],
                dst_ref=slots.at[me],
                send_sem=send.at[d],
                recv_sem=recv.at[me],
                device_id=device_of(p),
                device_id_type=MESH,
            )
            copy.start()
            copies.append(copy)
        for d, p in enumerate(peers):
            pltpu.make_async_remote_copy(
                src_ref=slots.at[p],
                dst_ref=slots.at[p],
                send_sem=send.at[d],
                recv_sem=recv.at[p],
                device_id=device_of(p),
                device_id_type=MESH,
            ).wait_recv()
        total = slots[0]
        for k in range(1, count):
            total = total + slots[k]
        return total, copies

    total, sent_gy = gather(mine, sum_gy, gy_send, gy_recv, gy, gy_peers, lambda p: (gx, p))
    total, sent_z = gather(total, sum_z, z_send, z_recv, zz, z_peers, lambda p: (yy * nz + p, gy))
    total, sent_y = gather(total, sum_y, y_send, y_recv, yy, y_peers, lambda p: (p * nz + zz, gy))

    def item(k):
        return total[0:1, k : k + 1]

    def solve(k11, k12, k22, k1, k2):
        scale = 1.0 / item(k11)
        a12, a22 = item(k12) * scale, item(k22) * scale
        f1, f2 = item(k1) * scale, item(k2) * scale
        det = 1.0 / (a22 - a12 * a12)
        return (a22 * f1 - a12 * f2) * det, (f2 - a12 * f1) * det

    c1, c2 = solve(0, 1, 2, 3, 4)
    d1, d2 = solve(5, 6, 7, 8, 9)
    velocity[0] = v_guess[0] + c1 * local[0] + c2 * local[3]
    velocity[1] = v_guess[1] + c1 * local[1] + c2 * local[4]
    level[...] = v_oguess[...] + d1 * local[2] + d2 * local[5]

    @pl.when(top)
    def _():
        fold[0].wait_send()

    for k in (1, 2):

        @pl.when(jnp.logical_and(top, jnp.logical_not(mirror_self[k - 1])))
        def _():
            fold[k].wait_send()

    @pl.when(jnp.logical_not(top))
    def _():
        for copy in up:
            copy.wait_send()

    @pl.when(jnp.logical_not(bottom))
    def _():
        for k in range(3):
            down[k].wait_send()

    to_east.wait_send()
    to_west.wait_send()
    for copy in sent_gy + sent_z + sent_y:
        copy.wait_send()


def build(mesh, ny, nz, interpret=False):
    ngy = mesh.shape["gy"]
    f32 = jnp.float32
    block = pltpu.VMEM((ROWS, COLS), f32)
    pair = pltpu.VMEM((2, ROWS, COLS), f32)
    whole = pltpu.VMEM((ROWS, COLS), jnp.int32)
    dma = pltpu.SemaphoreType.DMA

    def body(*args):
        return pl.pallas_call(
            functools.partial(kernel, (ny, nz, ngy)),
            out_shape=(
                jax.ShapeDtypeStruct((2, ROWS, COLS), f32),
                jax.ShapeDtypeStruct((ROWS, COLS), f32),
            ),
            in_specs=[pl.BlockSpec(memory_space=pl.ANY)] * 10,
            out_specs=(pl.BlockSpec(memory_space=pltpu.VMEM), pl.BlockSpec(memory_space=pltpu.VMEM)),
            scratch_shapes=[
                pair,
                pair,
                block,
                block,
                block,
                block,
                block,
                block,
                whole,
                whole,
                pltpu.VMEM((9, EXT_ROWS, EXT_COLS), f32),
                pltpu.VMEM((7, ROWS, COLS), f32),
                pltpu.VMEM((2, 5, 8, COLS), f32),
                pltpu.VMEM((2, 5, 8, COLS), f32),
                pltpu.VMEM((2, PACK, 128), f32),
                pltpu.VMEM((6, PACK, 128), f32),
                pltpu.VMEM((ngy, 1, 128), f32),
                pltpu.VMEM((nz, 1, 128), f32),
                pltpu.VMEM((ny, 1, 128), f32),
                dma((10,)),
                dma((8,)),
                dma((8,)),
                dma((ngy - 1,)),
                dma((ngy,)),
                dma((nz - 1,)),
                dma((nz,)),
                dma((ny - 1,)),
                dma((ny,)),
            ],
            compiler_params=pltpu.CompilerParams(collective_id=0, has_side_effects=True),
            name="picard",
        )(*args)

    both = P(None, "gx", "gy")
    one = P("gx", "gy")
    return jax.shard_map(
        body,
        mesh=mesh,
        in_specs=(both, both, one, one, one, one, one, one, one, one),
        out_specs=(both, one),
        check_vma=False,
    )


def solution(mesh):
    return build(mesh, 8, 12)
```

time: 388 us -> 44.6 us (0.11)
  the two profiles are of different devices: /device:TPU:1 before, /device:TPU:8 now
where the time goes in v1:
time: 44.6 us; the launch traced here: 44.4 us
  Pallas kernels  41.5 us (93%)
  local copies, waits for them, and re-layouts  2.23 us (5%)
  between operations  0.65 us (1%)
    pallas_call x1, Pallas kernels, body(): pl.pallas_call(functools.partial(kernel, (ny, nz, ngy)), out_shape=(jax.S...  41.5 us
    unnamed x4, local copies, waits for them, and re-layouts  2.23 us

profile of v1, /device:TPU:8, one launch (start us, length us, event | category | flops | bytes accessed | tf_op | source)
XLA Modules:
  0.0 44.4 jit_solution(3868669319551426723)
XLA Ops:
  0.6 41.5 %picard.1 = (f32[2,64,256]{2,1,0:T(8,128)}, f32[64,256]{1,0:T(8,128)}) custom-call(f32[2,64,256]{2,1,0:T(8,128)} %ice_rhs.1, f32[2,64,256]{2,1,0:T(8,128)} %ice_guess.1, f32[64,256]{1,0:T(8,128)} %ocean_rhs.1, f32[64,256]{1,0:T(8,128)} %ocean_guess.1, f32[64,256]{1,0:T(8,128)} %ice_diag.1, f32[64,256]{1,0:T(8,128)} %ice_visc.1, f32[64,256]{1,0:T(8,128)} %coriolis.1, ...), custom_call_target="tpu_custom_call" | custom-call | tf_op jit(solution)/shard_map/picard/pallas_call | solution.py:472
  42.2 0.0 copy-start
  42.2 1.6 %copy.14 = f32[2,64,256]{2,1,0:T(8,128)} copy(f32[2,64,256]{2,1,0:T(8,128)} %get-tuple-element.4) | data formatting | bytes 262144
  43.8 0.0 copy-done
  43.8 0.6 %copy.15 = f32[64,256]{1,0:T(8,128)} copy(f32[64,256]{1,0:T(8,128)S(1)} %copy-done) | data formatting | bytes 131072
Async XLA Ops:
  42.2 1.6 %copy-start = (f32[64,256]{1,0:T(8,128)S(1)}, f32[64,256]{1,0:T(8,128)}, u32[]{:S(2)}) copy-start(f32[64,256]{1,0:T(8,128)} %get-tuple-element.5) | copy-start | bytes 196612

commit v2 on v1

--- a/solution.py
+++ b/solution.py
@@ -10,8 +10,11 @@
 MESH = pl.DeviceIdType.MESH
 
 M_U, M_V, H_U, H_V, M_O, H_O, B_I, B_O, TURN = range(9)
-GROUPS = ((M_U, M_V, H_U, H_V, M_O), (H_O, B_I, B_O, TURN))
-PACK = 48
+DEPTH = {M_U: 3, M_V: 3, M_O: 3, H_U: 2, H_V: 2, H_O: 2, B_I: 2, B_O: 2, TURN: 1}
+HALVES = ((M_U, M_V, H_U, H_V), (M_O, H_O, B_I, B_O, TURN))
+TILES = ((M_U, M_V, H_U), (M_O, H_V, H_O, TURN), (B_I, B_O))
+PACK = 24
+HUBS = 4
 ROWS = 64
 COLS = 256
 EXT_ROWS = ROWS + 8
@@ -20,6 +23,47 @@
 
 def iota(shape, dim):
     return lax.broadcasted_iota(jnp.int32, shape, dim)
+
+
+def roll(x, by, dim):
+    size = x.shape[dim]
+    return x if by % size == 0 else pltpu.roll(x, by % size, dim)
+
+
+def columns():
+    for half, fields in enumerate(HALVES):
+        at = 0
+        for f in fields:
+            yield half, f, at, DEPTH[f]
+            at += 2 * DEPTH[f]
+
+
+def packed_rows():
+    for t, fields in enumerate(TILES):
+        at = 0
+        for f in fields:
+            yield t, f, at, DEPTH[f]
+            at += DEPTH[f]
+
+
+def northern_rows():
+    row, lane = iota((PACK, 128), 0), iota((PACK, 128), 1)
+    step = jnp.full((PACK, 128), -1, jnp.int32)
+    for half, _, at, n in columns():
+        here = (lane < 64) if half == 0 else (lane >= 64)
+        for k in range(n):
+            step = jnp.where(jnp.logical_and(here, row == at + n + k), k, step)
+    return step
+
+
+def corners(turned):
+    lane = lax.rem(iota((8, 128), 1) + 2, 64)
+    first, second, third = [roll(turned[8 * t : 8 * t + 8], 4 * t, 1) for t in range(3)]
+    return jnp.where(lane < 4, first, jnp.where(lane < 8, second, third))
+
+
+def from_corners(tile):
+    return jnp.concatenate([roll(tile, -4 * t, 1) for t in range(3)], axis=0)
 
 
 def around(q):
@@ -63,18 +107,15 @@
     zonal_in,
     merid_out,
     merid_in,
+    corner_out,
+    corner_in,
     sum_gy,
-    sum_z,
-    sum_y,
+    sum_plane,
+    result,
     load_sems,
     halo_send,
     halo_recv,
-    gy_send,
-    gy_recv,
-    z_send,
-    z_recv,
-    y_send,
-    y_recv,
+    sum_sems,
 ):
     ny, nz, ngy = sizes
     ngx = ny * nz
@@ -117,8 +158,11 @@
     norths = [north_of(step) for step in (0, 1, -1)]
     souths = [south_of(step) for step in (0, 1, -1)]
     gy_peers = [lax.rem(gy + d, ngy) for d in range(1, ngy)]
-    z_peers = [lax.rem(zz + d, nz) for d in range(1, nz)]
-    y_peers = [lax.rem(yy + d, ny) for d in range(1, ny)]
+    nhub = min(HUBS, nz - 1)
+    hubs = [y * nz + z for z in range(nhub) for y in range(ny)]
+    is_hub = zz < nhub
+    later = [z for z in range(nhub, nz)]
+    relay_of = {z: nhub - 1 if 2 * (z - nhub) < nz - nhub else 0 for z in later}
 
     barrier = pltpu.get_barrier_semaphore()
 
@@ -126,6 +170,9 @@
         pl.semaphore_signal(barrier, inc=1, device_id=device, device_id_type=MESH)
 
     mirror_self = [jnp.logical_and(top, norths[k][0] == gx) for k in (1, 2)]
+
+    for copy in loads:
+        copy.start()
 
     greet(norths[0])
     for k in (1, 2):
@@ -134,22 +181,21 @@
         def _():
             greet(norths[k])
 
-    for p in z_peers:
-        greet((yy * nz + p, gy))
-    for p in y_peers:
-        greet((p * nz + zz, gy))
+    greet(east)
+    greet(west)
     for p in gy_peers:
         greet((gx, p))
-    greet(east)
-    greet(west)
 
     @pl.when(jnp.logical_not(bottom))
     def _():
         for device in souths:
             greet(device)
 
-    for copy in loads:
-        copy.start()
+    @pl.when(is_hub)
+    def _():
+        for d in range(1, ngx):
+            greet((lax.rem(gx + d, ngx), gy))
+
     for copy in loads:
         copy.wait()
 
@@ -189,34 +235,35 @@
         fields[f, 0:ROWS, 0:COLS] = own[f]
 
     sub = iota((8, COLS), 0)
-    for t in range(5):
-        a, b = 2 * t, min(2 * t + 1, 8)
-        first_a, last_a = own[a][0:8], own[a][ROWS - 8 : ROWS]
-        first_b, last_b = own[b][0:8], own[b][ROWS - 8 : ROWS]
-        zonal_out[0, t] = jnp.where(sub >= 4, last_a, pltpu.roll(last_b, 3, 0))
-        zonal_out[1, t] = jnp.where(sub < 4, first_a, pltpu.roll(first_b, 5, 0))
+    eastward = [jnp.zeros((8, COLS), jnp.float32)] * len(TILES)
+    westward = [jnp.zeros((8, COLS), jnp.float32)] * len(TILES)
+    for t, f, at, n in packed_rows():
+        eastward[t] = jnp.where(
+            jnp.logical_and(sub >= 8 - at - n, sub < 8 - at), roll(own[f][ROWS - 8 : ROWS], -at, 0), eastward[t]
+        )
+        westward[t] = jnp.where(jnp.logical_and(sub >= at, sub < at + n), roll(own[f][0:8], at, 0), westward[t])
+    for t in range(len(TILES)):
+        zonal_out[0, t] = eastward[t]
+        zonal_out[1, t] = westward[t]
 
     lane = iota((ROWS, 128), 1)
-    halves = []
-    for group in GROUPS:
-        packed = jnp.zeros((ROWS, 128), jnp.float32)
-        for k, f in enumerate(group):
-            edge = jnp.where(lane < 64, own[f][:, 0:128], own[f][:, COLS - 128 : COLS])
-            moved = pltpu.roll(edge, 8 * (k + 1), 1)
-            packed = jnp.where(jnp.logical_and(lane >= 8 * k + 4, lane < 8 * k + 12), moved, packed)
-        halves.append(packed)
+    halves = [jnp.zeros((ROWS, 128), jnp.float32)] * 2
+    for half, f, at, n in columns():
+        edge = jnp.where(lane < 64, own[f][:, 0:128], own[f][:, COLS - 128 : COLS])
+        halves[half] = jnp.where(
+            jnp.logical_and(lane >= at, lane < at + 2 * n), roll(edge, at + n, 1), halves[half]
+        )
     turned = jnp.transpose(jnp.concatenate(halves, axis=0))[0:PACK]
     merid_out[0] = turned
     merid_out[1] = turned
+    corner_out[0] = corners(turned)
+    corner_out[1] = corners(turned)
 
     @pl.when(top)
     def _():
-        row = iota((PACK, 128), 0)
-        within = lax.rem(row, 8)
+        step = northern_rows()
         flipped = jnp.where(
-            within == 0,
-            pltpu.roll(turned, 1, 0),
-            jnp.where(within == 1, pltpu.roll(turned, 3, 0), pltpu.roll(turned, 5, 0)),
+            step == 0, roll(turned, 1, 0), jnp.where(step == 1, roll(turned, 3, 0), roll(turned, 5, 0))
         )
         swap = jnp.where(
             (iota((128, 128), 0) ^ iota((128, 128), 1)) == 63, 1.0, 0.0
@@ -224,15 +271,17 @@
         mirrored = jnp.dot(
             flipped, swap, precision=lax.Precision.HIGHEST, preferred_element_type=jnp.float32
         )
-        minus = jnp.logical_and(row < 40, iota((PACK, 128), 1) < 64)
-        merid_out[0] = jnp.where(minus, -mirrored, mirrored)
+        mirrored = jnp.where(iota((PACK, 128), 1) < 64, -mirrored, mirrored)
+        merid_out[0] = mirrored
+        corner_out[0] = corners(mirrored)
 
     @pl.when(bottom)
     def _():
-        for k in range(3):
-            merid_in[3 + k] = jnp.zeros((PACK, 128), jnp.float32)
-
-    expected = ny + nz + ngy - 3 + 2 + 1 + jnp.where(bottom, 0, 3)
+        merid_in[1] = jnp.zeros((PACK, 128), jnp.float32)
+        for k in (2, 3):
+            corner_in[k] = jnp.zeros((8, 128), jnp.float32)
+
+    expected = len(hubs) + ngy - 1 + 2 + 1 + jnp.where(bottom, 0, 3) - jnp.where(is_hub, 1, 0)
     for k in (1, 2):
         expected = expected + jnp.where(mirror_self[k - 1], 0, 1)
     pl.semaphore_wait(barrier, expected)
@@ -247,14 +296,20 @@
             device_id_type=MESH,
         )
 
-    slot_of = (0, 2, 1)
-    fold = [remote(merid_out.at[0], merid_in.at[k], k, k, norths[k]) for k in range(3)]
+    fold = [
+        remote(merid_out.at[0], merid_in.at[0], 0, 0, norths[0]),
+        remote(corner_out.at[0], corner_in.at[0], 1, 2, norths[1]),
+        remote(corner_out.at[0], corner_in.at[1], 2, 3, norths[2]),
+    ]
     up = [
-        remote(merid_out.at[0], merid_in.at[3 + slot_of[k]], k, 3 + slot_of[k], norths[k])
-        for k in range(3)
+        remote(merid_out.at[0], merid_in.at[1], 0, 1, norths[0]),
+        remote(corner_out.at[0], corner_in.at[3], 1, 5, norths[1]),
+        remote(corner_out.at[0], corner_in.at[2], 2, 4, norths[2]),
     ]
     down = [
-        remote(merid_out.at[1], merid_in.at[slot_of[k]], 3 + k, slot_of[k], souths[k]) for k in range(3)
+        remote(merid_out.at[1], merid_in.at[0], 3, 0, souths[0]),
+        remote(corner_out.at[1], corner_in.at[1], 4, 3, souths[1]),
+        remote(corner_out.at[1], corner_in.at[0], 5, 2, souths[2]),
     ]
     to_east = remote(zonal_out.at[0], zonal_in.at[0], 6, 6, east)
     to_west = remote(zonal_out.at[1], zonal_in.at[1], 7, 7, west)
@@ -271,7 +326,7 @@
 
         @pl.when(mirror_self[k - 1])
         def _():
-            merid_in[k] = merid_out[0]
+            corner_in[k - 1] = corner_out[0]
 
     @pl.when(jnp.logical_not(top))
     def _():
@@ -289,43 +344,43 @@
     to_east.wait_recv()
     to_west.wait_recv()
 
-    for t in range(5):
-        from_west = zonal_in[0, t]
-        from_east = zonal_in[1, t]
-        fields[2 * t, ROWS:EXT_ROWS, 0:COLS] = jnp.where(sub < 4, from_east, from_west)
-        if t < 4:
-            fields[2 * t + 1, ROWS:EXT_ROWS, 0:COLS] = jnp.where(
-                sub < 4, pltpu.roll(from_east, 3, 0), pltpu.roll(from_west, 5, 0)
-            )
-
-    def arrived(k):
-        remote(merid_out.at[0], merid_in.at[k], k, k, east).wait_recv()
-
-    arrived(0)
+    for t, f, at, n in packed_rows():
+        fields[f, ROWS:EXT_ROWS, 0:COLS] = jnp.where(
+            sub < 4, roll(zonal_in[1, t], -at, 0), roll(zonal_in[0, t], at, 0)
+        )
+
+    def arrived(k, src, dst):
+        remote(src, dst, k, k, east).wait_recv()
+
+    arrived(0, merid_out.at[0], merid_in.at[0])
     for k in (1, 2):
 
         @pl.when(jnp.logical_not(mirror_self[k - 1]))
         def _():
-            arrived(k)
+            arrived(1 + k, corner_out.at[0], corner_in.at[k - 1])
 
     @pl.when(jnp.logical_not(bottom))
     def _():
-        for k in range(3):
-            arrived(3 + k)
-
-    north_side = lax.rem(iota((PACK, 128), 0), 8) < 4
-    plane, from_e, from_w = [jnp.where(north_side, merid_in[k], merid_in[3 + k]) for k in range(3)]
+        arrived(1, merid_out.at[0], merid_in.at[1])
+        for k in (2, 3):
+            arrived(2 + k, corner_out.at[0], corner_in.at[k])
+
+    northern = northern_rows() >= 0
+    plane = jnp.where(northern, merid_in[0], merid_in[1])
+    from_e = jnp.where(northern, from_corners(corner_in[0]), from_corners(corner_in[2]))
+    from_w = jnp.where(northern, from_corners(corner_in[1]), from_corners(corner_in[3]))
     lane = iota((PACK, 128), 1)
     pad = jnp.zeros((128 - PACK, 128), jnp.float32)
-    for g, group in enumerate(GROUPS):
-        if g == 0:
-            center, right, left = plane, pltpu.roll(from_e, 64, 1), pltpu.roll(from_w, 8, 1)
+    backs = []
+    for half in range(2):
+        if half == 0:
+            center, right, left = plane, roll(from_e, 64, 1), roll(from_w, 8, 1)
         else:
-            center, right, left = pltpu.roll(plane, 64, 1), from_e, pltpu.roll(from_w, 72, 1)
+            center, right, left = roll(plane, 64, 1), from_e, roll(from_w, 72, 1)
         merged = jnp.where(lane < 64, center, jnp.where(lane < 68, right, left))
-        back = jnp.transpose(jnp.concatenate([merged, pad], axis=0))[0:EXT_ROWS]
-        for k, f in enumerate(group):
-            fields[f, :, COLS:EXT_COLS] = pltpu.roll(back, 128 - 8 * (k + 1), 1)
+        backs.append(jnp.transpose(jnp.concatenate([merged, pad], axis=0))[0:EXT_ROWS])
+    for half, f, at, n in columns():
+        fields[f, :, COLS:EXT_COLS] = roll(backs[half], -(at + n), 1)
 
     b_i = fields[B_I]
     b_o = fields[B_O]
@@ -385,38 +440,53 @@
     sums = jnp.sum(sums, axis=1, keepdims=True)
     mine = jnp.sum(jnp.where(row == iota((16, 128), 1), sums, 0.0), axis=0, keepdims=True)
 
-    def gather(value, slots, send, recv, me, peers, device_of):
-        count = len(peers) + 1
-        slots[me] = value
-        copies = []
-        for d, p in enumerate(peers):
-            copy = pltpu.make_async_remote_copy(
-                src_ref=slots.at[me],
-                dst_ref=slots.at[me],
-                send_sem=send.at[d],
-                recv_sem=recv.at[me],
-                device_id=device_of(p),
-                device_id_type=MESH,
-            )
-            copy.start()
-            copies.append(copy)
-        for d, p in enumerate(peers):
-            pltpu.make_async_remote_copy(
-                src_ref=slots.at[p],
-                dst_ref=slots.at[p],
-                send_sem=send.at[d],
-                recv_sem=recv.at[p],
-                device_id=device_of(p),
-                device_id_type=MESH,
-            ).wait_recv()
-        total = slots[0]
-        for k in range(1, count):
-            total = total + slots[k]
-        return total, copies
-
-    total, sent_gy = gather(mine, sum_gy, gy_send, gy_recv, gy, gy_peers, lambda p: (gx, p))
-    total, sent_z = gather(total, sum_z, z_send, z_recv, zz, z_peers, lambda p: (yy * nz + p, gy))
-    total, sent_y = gather(total, sum_y, y_send, y_recv, yy, y_peers, lambda p: (p * nz + zz, gy))
+    def rows_of(slots, count, sem):
+        return pltpu.make_async_copy(slots.at[pl.ds(0, count)], slots.at[pl.ds(0, count)], sem)
+
+    def send_row(slots, at, dst, dst_at, send, recv, device):
+        pltpu.make_async_remote_copy(
+            src_ref=slots.at[at],
+            dst_ref=dst.at[dst_at],
+            send_sem=sum_sems.at[send],
+            recv_sem=sum_sems.at[recv],
+            device_id=device,
+            device_id_type=MESH,
+        ).start()
+
+    sum_gy[gy] = mine
+    for p in gy_peers:
+        send_row(sum_gy, gy, sum_gy, gy, 0, 1, (gx, p))
+    rows_of(sum_gy, ngy - 1, sum_sems.at[1]).wait()
+    total = sum_gy[0]
+    for k in range(1, ngy):
+        total = total + sum_gy[k]
+
+    sum_plane[gx] = total
+    for hub in hubs:
+
+        @pl.when(gx != hub)
+        def _():
+            send_row(sum_plane, gx, sum_plane, gx, 2, 3, (hub, gy))
+
+    @pl.when(is_hub)
+    def _():
+        rows_of(sum_plane, ngx - 1, sum_sems.at[3]).wait()
+        whole = sum_plane[0]
+        for k in range(1, ngx):
+            whole = whole + sum_plane[k]
+        result[0] = whole
+        result[1] = whole
+        for z in later:
+
+            @pl.when(zz == relay_of[z])
+            def _():
+                send_row(result, 0, result, 1, 4, 5, (yy * nz + z, gy))
+
+    @pl.when(jnp.logical_not(is_hub))
+    def _():
+        rows_of(result, 1, sum_sems.at[5]).wait()
+
+    total = result[1]
 
     def item(k):
         return total[0:1, k : k + 1]
@@ -456,8 +526,23 @@
 
     to_east.wait_send()
     to_west.wait_send()
-    for copy in sent_gy + sent_z + sent_y:
-        copy.wait_send()
+    rows_of(sum_gy, ngy - 1, sum_sems.at[0]).wait()
+
+    @pl.when(is_hub)
+    def _():
+        rows_of(sum_plane, len(hubs) - 1, sum_sems.at[2]).wait()
+
+    @pl.when(jnp.logical_not(is_hub))
+    def _():
+        rows_of(sum_plane, len(hubs), sum_sems.at[2]).wait()
+
+    for hub in range(nhub):
+        served = len([z for z in later if relay_of[z] == hub])
+        if served:
+
+            @pl.when(zz == hub)
+            def _():
+                rows_of(sum_plane, served, sum_sems.at[4]).wait()
 
 
 def build(mesh, ny, nz, interpret=False):
@@ -472,8 +557,8 @@
         return pl.pallas_call(
             functools.partial(kernel, (ny, nz, ngy)),
             out_shape=(
-                jax.ShapeDtypeStruct((2, ROWS, COLS), f32),
-                jax.ShapeDtypeStruct((ROWS, COLS), f32),
+                pltpu.VMEM((2, ROWS, COLS), f32),
+                pltpu.VMEM((ROWS, COLS), f32),
             ),
             in_specs=[pl.BlockSpec(memory_space=pl.ANY)] * 10,
             out_specs=(pl.BlockSpec(memory_space=pltpu.VMEM), pl.BlockSpec(memory_space=pltpu.VMEM)),
@@ -490,26 +575,23 @@
                 whole,
                 pltpu.VMEM((9, EXT_ROWS, EXT_COLS), f32),
                 pltpu.VMEM((7, ROWS, COLS), f32),
-                pltpu.VMEM((2, 5, 8, COLS), f32),
-                pltpu.VMEM((2, 5, 8, COLS), f32),
+                pltpu.VMEM((2, 3, 8, COLS), f32),
+                pltpu.VMEM((2, 3, 8, COLS), f32),
                 pltpu.VMEM((2, PACK, 128), f32),
-                pltpu.VMEM((6, PACK, 128), f32),
+                pltpu.VMEM((2, PACK, 128), f32),
+                pltpu.VMEM((2, 8, 128), f32),
+                pltpu.VMEM((4, 8, 128), f32),
                 pltpu.VMEM((ngy, 1, 128), f32),
-                pltpu.VMEM((nz, 1, 128), f32),
-                pltpu.VMEM((ny, 1, 128), f32),
+                pltpu.VMEM((ny * nz, 1, 128), f32),
+                pltpu.VMEM((2, 1, 128), f32),
                 dma((10,)),
                 dma((8,)),
                 dma((8,)),
-                dma((ngy - 1,)),
-                dma((ngy,)),
-                dma((nz - 1,)),
-                dma((nz,)),
-                dma((ny - 1,)),
-                dma((ny,)),
+                dma((6,)),
             ],
-            compiler_params=pltpu.CompilerParams(collective_id=0, has_side_effects=True),
+            compiler_params=pltpu.CompilerParams(collective_id=0, has_side_effects=True, vmem_limit_bytes=16 * 1024 * 1024),
             name="picard",
-        )(*args)
+        )(*[pltpu.with_memory_space_constraint(a, pltpu.HBM) for a in args])
 
     both = P(None, "gx", "gy")
     one = P("gx", "gy")

time: 44.6 us -> 41 us (0.919)
  the two profiles are of different devices: /device:TPU:8 before, /device:TPU:1 now
where the time goes in v2:
time: 41 us; the launch traced here: 40.4 us
  Pallas kernels  38.4 us (94%)
  local copies, waits for them, and re-layouts  1.29 us (3%)
  between operations  0.64 us (2%)
    pallas_call x1, Pallas kernels, body(): pl.pallas_call(functools.partial(kernel, (ny, nz, ngy)), out_shape=(pltpu...  38.4 us
    unnamed x2, local copies, waits for them, and re-layouts  1.29 us

profile of v2, /device:TPU:1, one launch (start us, length us, event | category | flops | bytes accessed | tf_op | source)
XLA Modules:
  0.0 40.4 jit_solution(4986953505477430372)
XLA Ops:
  0.6 38.4 %picard.1 = (f32[2,64,256]{2,1,0:T(8,128)S(1)}, f32[64,256]{1,0:T(8,128)S(1)}) custom-call(f32[2,64,256]{2,1,0:T(8,128)} %ice_rhs.1, f32[2,64,256]{2,1,0:T(8,128)} %ice_guess.1, f32[64,256]{1,0:T(8,128)} %ocean_rhs.1, f32[64,256]{1,0:T(8,128)} %ocean_guess.1, f32[64,256]{1,0:T(8,128)} %ice_diag.1, f32[64,256]{1,0:T(8,128)} %ice_visc.1, f32[64,256]{1,0:T(8,128)} %coriolis.1, ...), custom_call_target="tpu_custom_call" | custom-call | tf_op jit(solution)/shard_map/picard/pallas_call | solution.py:557
  39.1 0.7 %copy.14 = f32[2,64,256]{2,1,0:T(8,128)} copy(f32[2,64,256]{2,1,0:T(8,128)S(1)} %get-tuple-element.2) | data formatting | bytes 262144
  39.7 0.6 %copy.15 = f32[64,256]{1,0:T(8,128)} copy(f32[64,256]{1,0:T(8,128)S(1)} %get-tuple-element.3) | data formatting | bytes 131072

commit v3 on v2

--- a/solution.py
+++ b/solution.py
@@ -14,6 +14,7 @@
 HALVES = ((M_U, M_V, H_U, H_V), (M_O, H_O, B_I, B_O, TURN))
 TILES = ((M_U, M_V, H_U), (M_O, H_V, H_O, TURN), (B_I, B_O))
 PACK = 24
+STRIP = PACK + 16
 HUBS = 4
 ROWS = 64
 COLS = 256
@@ -106,15 +107,18 @@
     zonal_out,
     zonal_in,
     merid_out,
-    merid_in,
     corner_out,
-    corner_in,
+    north_in,
+    south_in,
+    post_in,
     sum_gy,
     sum_plane,
     result,
     load_sems,
     halo_send,
     halo_recv,
+    post_send,
+    post_recv,
     sum_sems,
 ):
     ny, nz, ngy = sizes
@@ -162,22 +166,43 @@
     hubs = [y * nz + z for z in range(nhub) for y in range(ny)]
     is_hub = zz < nhub
     later = [z for z in range(nhub, nz)]
-    relay_of = {z: nhub - 1 if 2 * (z - nhub) < nz - nhub else 0 for z in later}
 
     barrier = pltpu.get_barrier_semaphore()
 
     def greet(device):
         pl.semaphore_signal(barrier, inc=1, device_id=device, device_id_type=MESH)
 
-    mirror_self = [jnp.logical_and(top, norths[k][0] == gx) for k in (1, 2)]
+    far_z = 2 * nz // 3
+    posts = {}
+    for z in range(nz // 2, nz):
+        posts.setdefault(0 if z >= far_z else nz - 1 - z, []).append(z)
+
+    def is_late(g):
+        return 2 * lax.rem(g, nz) >= nz
+
+    def post_of(g):
+        z = lax.rem(g, nz)
+        far = z >= far_z
+        return g - z + jnp.where(far, 0, nz - 1 - z), jnp.where(far, z - far_z, 0)
+
+    def mirrors(g):
+        return [ngx - 1 - wrap(g + step) for step in (0, 1, -1)]
+
+    late = is_late(gx)
+    mirror_self = [
+        jnp.logical_and(jnp.logical_and(top, jnp.logical_not(late)), norths[k][0] == gx) for k in range(3)
+    ]
 
     for copy in loads:
         copy.start()
 
-    greet(norths[0])
-    for k in (1, 2):
-
-        @pl.when(jnp.logical_not(mirror_self[k - 1]))
+    @pl.when(jnp.logical_and(top, late))
+    def _():
+        greet((post_of(gx)[0], gy))
+
+    for k in range(3):
+
+        @pl.when(jnp.logical_not(jnp.logical_or(jnp.logical_and(top, late), mirror_self[k])))
         def _():
             greet(norths[k])
 
@@ -190,6 +215,14 @@
     def _():
         for device in souths:
             greet(device)
+
+    for at, served in posts.items():
+
+        @pl.when(jnp.logical_and(top, zz == at))
+        def _():
+            for z in served:
+                for g in mirrors(yy * nz + z):
+                    greet((g, gy))
 
     @pl.when(is_hub)
     def _():
@@ -277,13 +310,13 @@
 
     @pl.when(bottom)
     def _():
-        merid_in[1] = jnp.zeros((PACK, 128), jnp.float32)
-        for k in (2, 3):
-            corner_in[k] = jnp.zeros((8, 128), jnp.float32)
-
-    expected = len(hubs) + ngy - 1 + 2 + 1 + jnp.where(bottom, 0, 3) - jnp.where(is_hub, 1, 0)
-    for k in (1, 2):
-        expected = expected + jnp.where(mirror_self[k - 1], 0, 1)
+        south_in[...] = jnp.zeros((STRIP, 128), jnp.float32)
+
+    expected = len(hubs) + ngy - 1 + 2 + 3 + jnp.where(bottom, 0, 3) - jnp.where(is_hub, 1, 0)
+    for k in range(3):
+        expected = expected - jnp.where(mirror_self[k], 1, 0)
+    for at, served in posts.items():
+        expected = expected + jnp.where(jnp.logical_and(top, zz == at), len(served), 0)
     pl.semaphore_wait(barrier, expected)
 
     def remote(src, dst, sent, got, device):
@@ -296,37 +329,51 @@
             device_id_type=MESH,
         )
 
-    fold = [
-        remote(merid_out.at[0], merid_in.at[0], 0, 0, norths[0]),
-        remote(corner_out.at[0], corner_in.at[0], 1, 2, norths[1]),
-        remote(corner_out.at[0], corner_in.at[1], 2, 3, norths[2]),
-    ]
+    parts = [pl.ds(0, PACK), pl.ds(PACK, 8), pl.ds(PACK + 8, 8)]
+    opposite = (0, 2, 1)
+    sources = [[merid_out.at[i], corner_out.at[i], corner_out.at[i]] for i in range(2)]
+    fold = [remote(sources[0][k], north_in.at[parts[k]], k, k, norths[k]) for k in range(3)]
     up = [
-        remote(merid_out.at[0], merid_in.at[1], 0, 1, norths[0]),
-        remote(corner_out.at[0], corner_in.at[3], 1, 5, norths[1]),
-        remote(corner_out.at[0], corner_in.at[2], 2, 4, norths[2]),
+        remote(sources[0][k], south_in.at[parts[opposite[k]]], k, 3 + opposite[k], norths[k])
+        for k in range(3)
     ]
     down = [
-        remote(merid_out.at[1], merid_in.at[0], 3, 0, souths[0]),
-        remote(corner_out.at[1], corner_in.at[1], 4, 3, souths[1]),
-        remote(corner_out.at[1], corner_in.at[0], 5, 2, souths[2]),
+        remote(sources[1][k], north_in.at[parts[opposite[k]]], 3 + k, opposite[k], souths[k])
+        for k in range(3)
     ]
+
+    def to_post(k):
+        post, slot = post_of(norths[k][0])
+        return pltpu.make_async_remote_copy(
+            src_ref=sources[0][k],
+            dst_ref=post_in.at[slot, parts[k]],
+            send_sem=halo_send.at[k],
+            recv_sem=post_recv.at[slot],
+            device_id=(post, gy),
+            device_id_type=MESH,
+        )
+
     to_east = remote(zonal_out.at[0], zonal_in.at[0], 6, 6, east)
     to_west = remote(zonal_out.at[1], zonal_in.at[1], 7, 7, west)
 
-    @pl.when(top)
-    def _():
-        fold[0].start()
-
-    for k in (1, 2):
-
-        @pl.when(jnp.logical_and(top, jnp.logical_not(mirror_self[k - 1])))
+    target_late = [is_late(norths[k][0]) for k in range(3)]
+    for k in range(3):
+
+        @pl.when(jnp.logical_and(top, target_late[k]))
+        def _():
+            to_post(k).start()
+
+        @pl.when(
+            jnp.logical_and(
+                jnp.logical_and(top, jnp.logical_not(target_late[k])), jnp.logical_not(mirror_self[k])
+            )
+        )
         def _():
             fold[k].start()
 
-        @pl.when(mirror_self[k - 1])
-        def _():
-            corner_in[k - 1] = corner_out[0]
+        @pl.when(mirror_self[k])
+        def _():
+            north_in[PACK + 8 * max(k - 1, 0) : PACK + 8 * max(k - 1, 0) + 8] = corner_out[0]
 
     @pl.when(jnp.logical_not(top))
     def _():
@@ -340,6 +387,22 @@
 
     to_east.start()
     to_west.start()
+
+    for at, served in posts.items():
+
+        @pl.when(jnp.logical_and(top, zz == at))
+        def _():
+            for slot, z in enumerate(served):
+                strip = post_in.at[slot]
+                pltpu.make_async_copy(strip, strip, post_recv.at[slot]).wait()
+                pltpu.make_async_remote_copy(
+                    src_ref=strip,
+                    dst_ref=north_in,
+                    send_sem=post_send.at[slot],
+                    recv_sem=halo_recv.at[0],
+                    device_id=(yy * nz + z, gy),
+                    device_id_type=MESH,
+                ).start()
 
     to_east.wait_recv()
     to_west.wait_recv()
@@ -349,26 +412,29 @@
             sub < 4, roll(zonal_in[1, t], -at, 0), roll(zonal_in[0, t], at, 0)
         )
 
-    def arrived(k, src, dst):
-        remote(src, dst, k, k, east).wait_recv()
-
-    arrived(0, merid_out.at[0], merid_in.at[0])
-    for k in (1, 2):
-
-        @pl.when(jnp.logical_not(mirror_self[k - 1]))
-        def _():
-            arrived(1 + k, corner_out.at[0], corner_in.at[k - 1])
-
-    @pl.when(jnp.logical_not(bottom))
-    def _():
-        arrived(1, merid_out.at[0], merid_in.at[1])
-        for k in (2, 3):
-            arrived(2 + k, corner_out.at[0], corner_in.at[k])
+    def arrived(k, dst):
+        pltpu.make_async_copy(dst, dst, halo_recv.at[k]).wait()
+
+    @pl.when(jnp.logical_and(top, late))
+    def _():
+        arrived(0, north_in)
+
+    for k in range(3):
+
+        @pl.when(jnp.logical_not(jnp.logical_or(jnp.logical_and(top, late), mirror_self[k])))
+        def _():
+            arrived(k, north_in.at[parts[k]])
+
+        @pl.when(jnp.logical_not(bottom))
+        def _():
+            arrived(3 + k, south_in.at[parts[k]])
 
     northern = northern_rows() >= 0
-    plane = jnp.where(northern, merid_in[0], merid_in[1])
-    from_e = jnp.where(northern, from_corners(corner_in[0]), from_corners(corner_in[2]))
-    from_w = jnp.where(northern, from_corners(corner_in[1]), from_corners(corner_in[3]))
+    plane = jnp.where(northern, north_in[0:PACK], south_in[0:PACK])
+    from_e, from_w = [
+        jnp.where(northern, from_corners(north_in[at : at + 8]), from_corners(south_in[at : at + 8]))
+        for at in (PACK, PACK + 8)
+    ]
     lane = iota((PACK, 128), 1)
     pad = jnp.zeros((128 - PACK, 128), jnp.float32)
     backs = []
@@ -478,7 +544,7 @@
         result[1] = whole
         for z in later:
 
-            @pl.when(zz == relay_of[z])
+            @pl.when(zz == nhub - 1)
             def _():
                 send_row(result, 0, result, 1, 4, 5, (yy * nz + z, gy))
 
@@ -504,15 +570,18 @@
     velocity[1] = v_guess[1] + c1 * local[1] + c2 * local[4]
     level[...] = v_oguess[...] + d1 * local[2] + d2 * local[5]
 
-    @pl.when(top)
-    def _():
-        fold[0].wait_send()
-
-    for k in (1, 2):
-
-        @pl.when(jnp.logical_and(top, jnp.logical_not(mirror_self[k - 1])))
+    for k in range(3):
+
+        @pl.when(jnp.logical_and(top, jnp.logical_not(mirror_self[k])))
         def _():
             fold[k].wait_send()
+
+    for at, served in posts.items():
+
+        @pl.when(jnp.logical_and(top, zz == at))
+        def _():
+            for slot, _ in enumerate(served):
+                pltpu.make_async_copy(post_in.at[slot], post_in.at[slot], post_send.at[slot]).wait()
 
     @pl.when(jnp.logical_not(top))
     def _():
@@ -536,13 +605,9 @@
     def _():
         rows_of(sum_plane, len(hubs), sum_sems.at[2]).wait()
 
-    for hub in range(nhub):
-        served = len([z for z in later if relay_of[z] == hub])
-        if served:
-
-            @pl.when(zz == hub)
-            def _():
-                rows_of(sum_plane, served, sum_sems.at[4]).wait()
+    @pl.when(zz == nhub - 1)
+    def _():
+        rows_of(sum_plane, len(later), sum_sems.at[4]).wait()
 
 
 def build(mesh, ny, nz, interpret=False):
@@ -578,15 +643,18 @@
                 pltpu.VMEM((2, 3, 8, COLS), f32),
                 pltpu.VMEM((2, 3, 8, COLS), f32),
                 pltpu.VMEM((2, PACK, 128), f32),
-                pltpu.VMEM((2, PACK, 128), f32),
                 pltpu.VMEM((2, 8, 128), f32),
-                pltpu.VMEM((4, 8, 128), f32),
+                pltpu.VMEM((STRIP, 128), f32),
+                pltpu.VMEM((STRIP, 128), f32),
+                pltpu.VMEM((nz - 2 * nz // 3, STRIP, 128), f32),
                 pltpu.VMEM((ngy, 1, 128), f32),
                 pltpu.VMEM((ny * nz, 1, 128), f32),
                 pltpu.VMEM((2, 1, 128), f32),
                 dma((10,)),
                 dma((8,)),
                 dma((8,)),
+                dma((nz - 2 * nz // 3,)),
+                dma((nz - 2 * nz // 3,)),
                 dma((6,)),
             ],
             compiler_params=pltpu.CompilerParams(collective_id=0, has_side_effects=True, vmem_limit_bytes=16 * 1024 * 1024),

time: 41 us -> 37.1 us (0.905); the launches traced: 40.4 us -> 37 us
  Pallas kernels: 38.4 us -> 35 us
    pallas_call x1, Pallas kernels: 38.4 us -> 35 us  [body(): pl.pallas_call(functools.partial(kernel, (ny, nz, ngy)), out_shape=(pltpu...]
where the time goes in v3:
time: 37.1 us; the launch traced here: 37 us
  Pallas kernels  35 us (94%)
  local copies, waits for them, and re-layouts  1.29 us (3%)
  between operations  0.64 us (2%)
    pallas_call x1, Pallas kernels, body(): pl.pallas_call(functools.partial(kernel, (ny, nz, ngy)), out_shape=(pltpu...  35 us
    unnamed x2, local copies, waits for them, and re-layouts  1.29 us

profile of v3, /device:TPU:1, one launch (start us, length us, event | category | flops | bytes accessed | tf_op | source)
XLA Modules:
  0.0 37.0 jit_solution(16220045408521408970)
XLA Ops:
  0.6 35.0 %picard.1 = (f32[2,64,256]{2,1,0:T(8,128)S(1)}, f32[64,256]{1,0:T(8,128)S(1)}) custom-call(f32[2,64,256]{2,1,0:T(8,128)} %ice_rhs.1, f32[2,64,256]{2,1,0:T(8,128)} %ice_guess.1, f32[64,256]{1,0:T(8,128)} %ocean_rhs.1, f32[64,256]{1,0:T(8,128)} %ocean_guess.1, f32[64,256]{1,0:T(8,128)} %ice_diag.1, f32[64,256]{1,0:T(8,128)} %ice_visc.1, f32[64,256]{1,0:T(8,128)} %coriolis.1, ...), custom_call_target="tpu_custom_call" | custom-call | tf_op jit(solution)/shard_map/picard/pallas_call | solution.py:622
  35.7 0.7 %copy.14 = f32[2,64,256]{2,1,0:T(8,128)} copy(f32[2,64,256]{2,1,0:T(8,128)S(1)} %get-tuple-element.2) | data formatting | bytes 262144
  36.3 0.6 %copy.15 = f32[64,256]{1,0:T(8,128)} copy(f32[64,256]{1,0:T(8,128)S(1)} %get-tuple-element.3) | data formatting | bytes 131072

commit v4 on v3

--- a/solution.py
+++ b/solution.py
@@ -111,6 +111,8 @@
     north_in,
     south_in,
     post_in,
+    seam_in,
+    seam_corner,
     sum_gy,
     sum_plane,
     result,
@@ -119,6 +121,8 @@
     halo_recv,
     post_send,
     post_recv,
+    seam_send,
+    seam_recv,
     sum_sems,
 ):
     ny, nz, ngy = sizes
@@ -172,23 +176,29 @@
     def greet(device):
         pl.semaphore_signal(barrier, inc=1, device_id=device, device_id_type=MESH)
 
-    far_z = 2 * nz // 3
+    half_z, far_z = nz // 2, 3 * nz // 4
     posts = {}
-    for z in range(nz // 2, nz):
-        posts.setdefault(0 if z >= far_z else nz - 1 - z, []).append(z)
+    for z in range(half_z, nz):
+        posts.setdefault(0 if z >= far_z else half_z - 1 - (z - half_z) % 2, []).append(z)
+    post_plane = gy == ngy - 2
 
     def is_late(g):
-        return 2 * lax.rem(g, nz) >= nz
+        return lax.rem(g, nz) >= half_z
 
     def post_of(g):
         z = lax.rem(g, nz)
         far = z >= far_z
-        return g - z + jnp.where(far, 0, nz - 1 - z), jnp.where(far, z - far_z, 0)
+        at = jnp.where(far, 0, half_z - 1 - lax.rem(z + nz - half_z, 2))
+        return g - z + at, jnp.where(far, z - far_z, (z - half_z) // 2)
 
     def mirrors(g):
         return [ngx - 1 - wrap(g + step) for step in (0, 1, -1)]
 
     late = is_late(gx)
+    seam_source = jnp.logical_and(top, zz == 0)
+    seam_post = jnp.logical_and(post_plane, zz == 0)
+    seam_target = jnp.logical_and(top, zz == nz - 1)
+    seam_diagonal = jnp.logical_and(post_plane, zz == nz - 1)
     mirror_self = [
         jnp.logical_and(jnp.logical_and(top, jnp.logical_not(late)), norths[k][0] == gx) for k in range(3)
     ]
@@ -198,15 +208,30 @@
 
     @pl.when(jnp.logical_and(top, late))
     def _():
-        greet((post_of(gx)[0], gy))
+        greet((post_of(gx)[0], gy - 1))
 
     for k in range(3):
 
-        @pl.when(jnp.logical_not(jnp.logical_or(jnp.logical_and(top, late), mirror_self[k])))
+        elsewhere = jnp.logical_or(jnp.logical_and(top, late), mirror_self[k])
+        if k == 1:
+            elsewhere = jnp.logical_or(elsewhere, seam_diagonal)
+
+        @pl.when(jnp.logical_not(elsewhere))
         def _():
             greet(norths[k])
 
-    greet(east)
+    @pl.when(seam_diagonal)
+    def _():
+        greet((gx - zz, gy))
+
+    @pl.when(seam_post)
+    def _():
+        greet((wrap(gx + nz), gy + 1))
+
+    @pl.when(jnp.logical_not(seam_target))
+    def _():
+        greet(east)
+
     greet(west)
     for p in gy_peers:
         greet((gx, p))
@@ -218,11 +243,11 @@
 
     for at, served in posts.items():
 
-        @pl.when(jnp.logical_and(top, zz == at))
+        @pl.when(jnp.logical_and(post_plane, zz == at))
         def _():
             for z in served:
                 for g in mirrors(yy * nz + z):
-                    greet((g, gy))
+                    greet((g, gy + 1))
 
     @pl.when(is_hub)
     def _():
@@ -316,7 +341,8 @@
     for k in range(3):
         expected = expected - jnp.where(mirror_self[k], 1, 0)
     for at, served in posts.items():
-        expected = expected + jnp.where(jnp.logical_and(top, zz == at), len(served), 0)
+        expected = expected + jnp.where(jnp.logical_and(post_plane, zz == at), len(served), 0)
+    expected = expected + jnp.where(seam_post, 1, 0) - jnp.where(seam_source, 1, 0)
     pl.semaphore_wait(barrier, expected)
 
     def remote(src, dst, sent, got, device):
@@ -349,48 +375,29 @@
             dst_ref=post_in.at[slot, parts[k]],
             send_sem=halo_send.at[k],
             recv_sem=post_recv.at[slot],
-            device_id=(post, gy),
+            device_id=(post, gy - 1),
             device_id_type=MESH,
         )
 
     to_east = remote(zonal_out.at[0], zonal_in.at[0], 6, 6, east)
     to_west = remote(zonal_out.at[1], zonal_in.at[1], 7, 7, west)
 
-    target_late = [is_late(norths[k][0]) for k in range(3)]
-    for k in range(3):
-
-        @pl.when(jnp.logical_and(top, target_late[k]))
-        def _():
-            to_post(k).start()
-
-        @pl.when(
-            jnp.logical_and(
-                jnp.logical_and(top, jnp.logical_not(target_late[k])), jnp.logical_not(mirror_self[k])
-            )
-        )
-        def _():
-            fold[k].start()
-
-        @pl.when(mirror_self[k])
-        def _():
-            north_in[PACK + 8 * max(k - 1, 0) : PACK + 8 * max(k - 1, 0) + 8] = corner_out[0]
-
-    @pl.when(jnp.logical_not(top))
-    def _():
-        for copy in up:
-            copy.start()
-
-    @pl.when(jnp.logical_not(bottom))
-    def _():
-        for copy in down:
-            copy.start()
-
-    to_east.start()
-    to_west.start()
+    def from_seam(src, dst, i, recv, there):
+        return pltpu.make_async_remote_copy(
+            src_ref=src,
+            dst_ref=dst,
+            send_sem=seam_send.at[i],
+            recv_sem=halo_recv.at[recv],
+            device_id=(gx - zz + nz - 1, there),
+            device_id_type=MESH,
+        )
+
+    seam_rows = from_seam(seam_in, zonal_in.at[1], 0, 7, gy + 1)
+    seam_tile = from_seam(seam_corner, north_in.at[parts[1]], 1, 1, gy)
 
     for at, served in posts.items():
 
-        @pl.when(jnp.logical_and(top, zz == at))
+        @pl.when(jnp.logical_and(post_plane, zz == at))
         def _():
             for slot, z in enumerate(served):
                 strip = post_in.at[slot]
@@ -400,9 +407,68 @@
                     dst_ref=north_in,
                     send_sem=post_send.at[slot],
                     recv_sem=halo_recv.at[0],
-                    device_id=(yy * nz + z, gy),
+                    device_id=(yy * nz + z, gy + 1),
                     device_id_type=MESH,
                 ).start()
+            if at == 0:
+                pltpu.make_async_copy(seam_in, seam_in, seam_recv.at[0]).wait()
+                seam_rows.start()
+                pltpu.make_async_copy(seam_corner, seam_corner, seam_recv.at[1]).wait()
+                seam_tile.start()
+
+    target_late = [is_late(norths[k][0]) for k in range(3)]
+    for k in range(3):
+
+        @pl.when(jnp.logical_and(top, target_late[k]))
+        def _():
+            to_post(k).start()
+
+        @pl.when(
+            jnp.logical_and(
+                jnp.logical_and(top, jnp.logical_not(target_late[k])), jnp.logical_not(mirror_self[k])
+            )
+        )
+        def _():
+            fold[k].start()
+
+        @pl.when(mirror_self[k])
+        def _():
+            north_in[PACK + 8 * max(k - 1, 0) : PACK + 8 * max(k - 1, 0) + 8] = corner_out[0]
+
+    @pl.when(jnp.logical_not(top))
+    def _():
+        for copy in up:
+            copy.start()
+
+    @pl.when(jnp.logical_not(bottom))
+    def _():
+        for copy in down[0:2]:
+            copy.start()
+
+    def to_seam(src, dst, sent, i):
+        return pltpu.make_async_remote_copy(
+            src_ref=src,
+            dst_ref=dst,
+            send_sem=halo_send.at[sent],
+            recv_sem=seam_recv.at[i],
+            device_id=(wrap(gx - nz), gy - 1),
+            device_id_type=MESH,
+        )
+
+    @pl.when(seam_source)
+    def _():
+        to_seam(zonal_out.at[1], seam_in, 7, 0).start()
+        to_seam(corner_out.at[1], seam_corner, 5, 1).start()
+
+    @pl.when(jnp.logical_not(seam_source))
+    def _():
+        to_west.start()
+
+    @pl.when(jnp.logical_not(jnp.logical_or(bottom, seam_source)))
+    def _():
+        down[2].start()
+
+    to_east.start()
 
     to_east.wait_recv()
     to_west.wait_recv()
@@ -578,10 +644,13 @@
 
     for at, served in posts.items():
 
-        @pl.when(jnp.logical_and(top, zz == at))
+        @pl.when(jnp.logical_and(post_plane, zz == at))
         def _():
             for slot, _ in enumerate(served):
                 pltpu.make_async_copy(post_in.at[slot], post_in.at[slot], post_send.at[slot]).wait()
+            if at == 0:
+                seam_rows.wait_send()
+                seam_tile.wait_send()
 
     @pl.when(jnp.logical_not(top))
     def _():
@@ -617,6 +686,7 @@
     pair = pltpu.VMEM((2, ROWS, COLS), f32)
     whole = pltpu.VMEM((ROWS, COLS), jnp.int32)
     dma = pltpu.SemaphoreType.DMA
+    slots = max(nz - 3 * nz // 4, (3 * nz // 4 - nz // 2 + 1) // 2)
 
     def body(*args):
         return pl.pallas_call(
@@ -646,15 +716,19 @@
                 pltpu.VMEM((2, 8, 128), f32),
                 pltpu.VMEM((STRIP, 128), f32),
                 pltpu.VMEM((STRIP, 128), f32),
-                pltpu.VMEM((nz - 2 * nz // 3, STRIP, 128), f32),
+                pltpu.VMEM((slots, STRIP, 128), f32),
+                pltpu.VMEM((3, 8, COLS), f32),
+                pltpu.VMEM((8, 128), f32),
                 pltpu.VMEM((ngy, 1, 128), f32),
                 pltpu.VMEM((ny * nz, 1, 128), f32),
                 pltpu.VMEM((2, 1, 128), f32),
                 dma((10,)),
                 dma((8,)),
                 dma((8,)),
-                dma((nz - 2 * nz // 3,)),
-                dma((nz - 2 * nz // 3,)),
+                dma((slots,)),
+                dma((slots,)),
+                dma((2,)),
+                dma((2,)),
                 dma((6,)),
             ],
             compiler_params=pltpu.CompilerParams(collective_id=0, has_side_effects=True, vmem_limit_bytes=16 * 1024 * 1024),

time: 37.1 us -> 40.2 us (1.084)
  Pallas kernels: 35 us -> 38.1 us
    pallas_call x1, Pallas kernels: 35 us -> 38.1 us  [body(): pl.pallas_call(functools.partial(kernel, (ny, nz, ngy)), out_shape=(pltpu...]
where the time goes in v4:
time: 40.2 us; the launch traced here: 40 us
  Pallas kernels  38.1 us (95%)
  local copies, waits for them, and re-layouts  1.29 us (3%)
  between operations  0.64 us (2%)
    pallas_call x1, Pallas kernels, body(): pl.pallas_call(functools.partial(kernel, (ny, nz, ngy)), out_shape=(pltpu...  38.1 us
    unnamed x2, local copies, waits for them, and re-layouts  1.29 us

profile of v4, /device:TPU:1, one launch (start us, length us, event | category | flops | bytes accessed | tf_op | source)
XLA Modules:
  0.0 40.0 jit_solution(13677539499186571720)
XLA Ops:
  0.6 38.1 %picard.1 = (f32[2,64,256]{2,1,0:T(8,128)S(1)}, f32[64,256]{1,0:T(8,128)S(1)}) custom-call(f32[2,64,256]{2,1,0:T(8,128)} %ice_rhs.1, f32[2,64,256]{2,1,0:T(8,128)} %ice_guess.1, f32[64,256]{1,0:T(8,128)} %ocean_rhs.1, f32[64,256]{1,0:T(8,128)} %ocean_guess.1, f32[64,256]{1,0:T(8,128)} %ice_diag.1, f32[64,256]{1,0:T(8,128)} %ice_visc.1, f32[64,256]{1,0:T(8,128)} %coriolis.1, ...), custom_call_target="tpu_custom_call" | custom-call | tf_op jit(solution)/shard_map/picard/pallas_call | solution.py:692
  38.7 0.7 %copy.14 = f32[2,64,256]{2,1,0:T(8,128)} copy(f32[2,64,256]{2,1,0:T(8,128)S(1)} %get-tuple-element.2) | data formatting | bytes 262144
  39.4 0.6 %copy.15 = f32[64,256]{1,0:T(8,128)} copy(f32[64,256]{1,0:T(8,128)S(1)} %get-tuple-element.3) | data formatting | bytes 131072

commit v5 on v3

--- a/solution.py
+++ b/solution.py
@@ -610,6 +610,17 @@
         rows_of(sum_plane, len(later), sum_sems.at[4]).wait()
 
 
+def put_out(velocity, level, velocity_out, level_out, sems):
+    copies = [
+        pltpu.make_async_copy(velocity, velocity_out, sems.at[0]),
+        pltpu.make_async_copy(level, level_out, sems.at[1]),
+    ]
+    for copy in copies:
+        copy.start()
+    for copy in copies:
+        copy.wait()
+
+
 def build(mesh, ny, nz, interpret=False):
     ngy = mesh.shape["gy"]
     f32 = jnp.float32
@@ -619,7 +630,7 @@
     dma = pltpu.SemaphoreType.DMA
 
     def body(*args):
-        return pl.pallas_call(
+        solved = pl.pallas_call(
             functools.partial(kernel, (ny, nz, ngy)),
             out_shape=(
                 pltpu.VMEM((2, ROWS, COLS), f32),
@@ -660,6 +671,15 @@
             compiler_params=pltpu.CompilerParams(collective_id=0, has_side_effects=True, vmem_limit_bytes=16 * 1024 * 1024),
             name="picard",
         )(*[pltpu.with_memory_space_constraint(a, pltpu.HBM) for a in args])
+        return pl.pallas_call(
+            put_out,
+            out_shape=(pltpu.HBM((2, ROWS, COLS), f32), pltpu.HBM((ROWS, COLS), f32)),
+            in_specs=[pl.BlockSpec(memory_space=pltpu.VMEM)] * 2,
+            out_specs=(pl.BlockSpec(memory_space=pltpu.HBM), pl.BlockSpec(memory_space=pltpu.HBM)),
+            scratch_shapes=[dma((2,))],
+            compiler_params=pltpu.CompilerParams(vmem_limit_bytes=4 * 1024 * 1024),
+            name="put_out",
+        )(*[pltpu.with_memory_space_constraint(a, pltpu.VMEM) for a in solved])
 
     both = P(None, "gx", "gy")
     one = P("gx", "gy")

time: 37.1 us -> 36.5 us (0.984)
  local copies, waits for them, and re-layouts: 1.29 us -> 0 us
  Pallas kernels: 35 us -> 35.7 us
    unnamed x2 -> x0, local copies, waits for them, and re-layouts: 1.29 us -> none
    pallas_call x0 -> x1, Pallas kernels: none -> 0.69 us  [body(): pl.pallas_call(put_out, out_shape=(pltpu.HBM((2, ROWS, COLS), f32), pltpu...]
where the time goes in v5:
time: 36.5 us; the launch traced here: 36.4 us
  Pallas kernels  35.7 us (98%)
  between operations  0.64 us (2%)
    pallas_call x1, Pallas kernels, body(): pl.pallas_call(functools.partial(kernel, (ny, nz, ngy)), out_shape=(pltpu...  35 us

profile of v5, /device:TPU:1, one launch (start us, length us, event | category | flops | bytes accessed | tf_op | source)
XLA Modules:
  0.0 36.4 jit_solution(8629631750896767382)
XLA Ops:
  0.6 35.0 %picard.1 = (f32[2,64,256]{2,1,0:T(8,128)S(1)}, f32[64,256]{1,0:T(8,128)S(1)}) custom-call(f32[2,64,256]{2,1,0:T(8,128)} %ice_rhs.1, f32[2,64,256]{2,1,0:T(8,128)} %ice_guess.1, f32[64,256]{1,0:T(8,128)} %ocean_rhs.1, f32[64,256]{1,0:T(8,128)} %ocean_guess.1, f32[64,256]{1,0:T(8,128)} %ice_diag.1, f32[64,256]{1,0:T(8,128)} %ice_visc.1, f32[64,256]{1,0:T(8,128)} %coriolis.1, ...), custom_call_target="tpu_custom_call" | custom-call | tf_op jit(solution)/shard_map/picard/pallas_call | solution.py:633
  35.7 0.7 %put_out.1 = (f32[2,64,256]{2,1,0:T(8,128)}, f32[64,256]{1,0:T(8,128)}) custom-call(f32[2,64,256]{2,1,0:T(8,128)S(1)} %get-tuple-element.4.velocity, f32[64,256]{1,0:T(8,128)S(1)} %get-tuple-element.5.level), custom_call_target="tpu_custom_call" | custom-call | tf_op jit(solution)/shard_map/put_out/pallas_call | solution.py:674

commit v6 on v5

--- a/solution.py
+++ b/solution.py
@@ -196,6 +196,20 @@
     for copy in loads:
         copy.start()
 
+    @pl.when(is_hub)
+    def _():
+        for z in sorted(range(nz), key=lambda z: abs(z - nz // 3)):
+            for d in sorted(range(ny), key=lambda d: -min(d, ny - d)):
+                there = (lax.rem(yy + d, ny) * nz + z, gy)
+                if d == 0 and z < nhub:
+
+                    @pl.when(zz != z)
+                    def _():
+                        greet(there)
+
+                else:
+                    greet(there)
+
     @pl.when(jnp.logical_and(top, late))
     def _():
         greet((post_of(gx)[0], gy))
@@ -223,11 +237,6 @@
             for z in served:
                 for g in mirrors(yy * nz + z):
                     greet((g, gy))
-
-    @pl.when(is_hub)
-    def _():
-        for d in range(1, ngx):
-            greet((lax.rem(gx + d, ngx), gy))
 
     for copy in loads:
         copy.wait()
@@ -537,9 +546,12 @@
     @pl.when(is_hub)
     def _():
         rows_of(sum_plane, ngx - 1, sum_sems.at[3]).wait()
-        whole = sum_plane[0]
-        for k in range(1, ngx):
-            whole = whole + sum_plane[k]
+        parts_of = [sum_plane[k] for k in range(8)]
+        for k in range(8, ngx):
+            parts_of[k % 8] = parts_of[k % 8] + sum_plane[k]
+        while len(parts_of) > 1:
+            parts_of = [a + b for a, b in zip(parts_of[0::2], parts_of[1::2])]
+        whole = parts_of[0]
         result[0] = whole
         result[1] = whole
         for z in later:

time: 36.5 us -> 36.5 us (level)
  no operation moved by 1% of the time
where the time goes in v6:
time: 36.5 us; the launch traced here: 36.3 us
  Pallas kernels  35.7 us (98%)
  between operations  0.64 us (2%)
    pallas_call x1, Pallas kernels, body(): pl.pallas_call(functools.partial(kernel, (ny, nz, ngy)), out_shape=(pltpu...  35 us

profile of v6, /device:TPU:1, one launch (start us, length us, event | category | flops | bytes accessed | tf_op | source)
XLA Modules:
  0.0 36.3 jit_solution(5323353396430520471)
XLA Ops:
  0.6 35.0 %picard.1 = (f32[2,64,256]{2,1,0:T(8,128)S(1)}, f32[64,256]{1,0:T(8,128)S(1)}) custom-call(f32[2,64,256]{2,1,0:T(8,128)} %ice_rhs.1, f32[2,64,256]{2,1,0:T(8,128)} %ice_guess.1, f32[64,256]{1,0:T(8,128)} %ocean_rhs.1, f32[64,256]{1,0:T(8,128)} %ocean_guess.1, f32[64,256]{1,0:T(8,128)} %ice_diag.1, f32[64,256]{1,0:T(8,128)} %ice_visc.1, f32[64,256]{1,0:T(8,128)} %coriolis.1, ...), custom_call_target="tpu_custom_call" | custom-call | tf_op jit(solution)/shard_map/picard/pallas_call | solution.py:645
  35.6 0.7 %put_out.1 = (f32[2,64,256]{2,1,0:T(8,128)}, f32[64,256]{1,0:T(8,128)}) custom-call(f32[2,64,256]{2,1,0:T(8,128)S(1)} %get-tuple-element.4.velocity, f32[64,256]{1,0:T(8,128)S(1)} %get-tuple-element.5.level), custom_call_target="tpu_custom_call" | custom-call | tf_op jit(solution)/shard_map/put_out/pallas_call | solution.py:686

commit v7 on v6

--- a/solution.py
+++ b/solution.py
@@ -445,7 +445,8 @@
         for at in (PACK, PACK + 8)
     ]
     lane = iota((PACK, 128), 1)
-    pad = jnp.zeros((128 - PACK, 128), jnp.float32)
+    pad = jnp.zeros((32 - PACK, 128), jnp.float32)
+    blank = jnp.zeros((EXT_ROWS, 96), jnp.float32)
     backs = []
     for half in range(2):
         if half == 0:
@@ -453,7 +454,8 @@
         else:
             center, right, left = roll(plane, 64, 1), from_e, roll(from_w, 72, 1)
         merged = jnp.where(lane < 64, center, jnp.where(lane < 68, right, left))
-        backs.append(jnp.transpose(jnp.concatenate([merged, pad], axis=0))[0:EXT_ROWS])
+        back = jnp.transpose(jnp.concatenate([merged, pad], axis=0))[0:EXT_ROWS]
+        backs.append(jnp.concatenate([back, blank], axis=1))
     for half, f, at, n in columns():
         fields[f, :, COLS:EXT_COLS] = roll(backs[half], -(at + n), 1)
 

time: 36.5 us -> 36.5 us (level)
  no operation moved by 1% of the time
where the time goes in v7:
time: 36.5 us; the launch traced here: 36.3 us
  Pallas kernels  35.7 us (98%)
  between operations  0.64 us (2%)
    pallas_call x1, Pallas kernels, body(): pl.pallas_call(functools.partial(kernel, (ny, nz, ngy)), out_shape=(pltpu...  35 us

profile of v7, /device:TPU:1, one launch (start us, length us, event | category | flops | bytes accessed | tf_op | source)
XLA Modules:
  0.0 36.3 jit_solution(18071511043071514340)
XLA Ops:
  0.6 35.0 %picard.1 = (f32[2,64,256]{2,1,0:T(8,128)S(1)}, f32[64,256]{1,0:T(8,128)S(1)}) custom-call(f32[2,64,256]{2,1,0:T(8,128)} %ice_rhs.1, f32[2,64,256]{2,1,0:T(8,128)} %ice_guess.1, f32[64,256]{1,0:T(8,128)} %ocean_rhs.1, f32[64,256]{1,0:T(8,128)} %ocean_guess.1, f32[64,256]{1,0:T(8,128)} %ice_diag.1, f32[64,256]{1,0:T(8,128)} %ice_visc.1, f32[64,256]{1,0:T(8,128)} %coriolis.1, ...), custom_call_target="tpu_custom_call" | custom-call | tf_op jit(solution)/shard_map/picard/pallas_call | solution.py:647
  35.6 0.7 %put_out.1 = (f32[2,64,256]{2,1,0:T(8,128)}, f32[64,256]{1,0:T(8,128)}) custom-call(f32[2,64,256]{2,1,0:T(8,128)S(1)} %get-tuple-element.4.velocity, f32[64,256]{1,0:T(8,128)S(1)} %get-tuple-element.5.level), custom_call_target="tpu_custom_call" | custom-call | tf_op jit(solution)/shard_map/put_out/pallas_call | solution.py:688
